TPU v7x, 32 devices: a whole 2x2x4 slice. The times are simulated.
32 devices in a mesh: ga: 8 (over z, core), gp: 4 (over y, x).
Axes of the slice: x: 2, y: 2, z: 4, core: 2. Of those that a mesh axis runs over, the one named last changes fastest.
Arguments:
- matel: bfloat16 [16, 16, 100352], P('ga', None, 'gp'), may hold values from -0.01953125 to 0.01953125
- pole_amp: bfloat16 [1024, 100352], P('ga', 'gp'), may hold values from -6 to 6
- pole_freq: bfloat16 [1024, 100352], P('ga', 'gp'), may hold values from 0.5 to 4
- band_energy: float32 [16], replicated, may hold values from -3 to 3
- energies: float32 [3], replicated, may hold values from -2 to 2
- owner: int32 [5], replicated, may hold values from 0 to 7
- slot: int32 [5], replicated, may hold values from 0 to 1
Outputs:
- sigma: float32 [3, 16, 16], replicated
Inputs may be any that keep to these rules, and one draw needn't show every extreme that they name: `slot`: position among the 2 bands stored by that row.
All inputs are finite; a program needn't handle non-finite values.
Results may differ from a plain program's by a relative error of at most 0.0029.
Values may be sent and summed in bfloat16 or wider, within the bound.
No kernel may reach another device: no remote copies, remote signals or barrier semaphores. Data moves between devices by JAX's collectives and lax.ppermute only.
A program may use at most 128 MiB of HBM per device.

v0:
```python
import functools

import jax
import jax.numpy as jnp
from jax import lax
from jax.experimental import pallas as pl
from jax.experimental.pallas import tpu as pltpu
from jax.sharding import PartitionSpec as P


FOLD_FLOPS = 48 * 10**9


def flip(values, axis, size, bit):
    return lax.ppermute(values, axis, [(i, i ^ bit) for i in range(size)])


def gather_sum(total, axis, size, bit, stop):
    while bit < size and bit <= stop:
        if 2 * bit < size and 2 * bit <= stop:
            parts = [flip(total, axis, size, mask) for mask in (bit, 2 * bit, 3 * bit)]
            total = (total + parts[0]) + (parts[1] + parts[2])
            bit *= 4
        else:
            total = total + flip(total, axis, size, bit)
            bit *= 2
    return total


def tile_width(cols, most):
    best = 128
    for count in range(1, most // 128 + 1):
        if cols % (128 * count) == 0:
            best = 128 * count
    return best


def fold_kernel(index_ref, detuning_ref, rows_ref, amp_ref, freq_ref, out_ref, *, inner):
    bands = out_ref.shape[0]
    states = rows_ref.shape[1]
    energies = out_ref.shape[1] // states

    def step(tile, carry):
        columns = pl.ds(pl.multiple_of(tile * inner, inner), inner)
        frequency = freq_ref[:, columns].astype(jnp.float32)
        numerator = amp_ref[:, columns].astype(jnp.float32) * frequency
        squared = frequency * frequency
        for band in range(bands):
            rows = rows_ref[index_ref[band]]
            for energy in range(energies):
                pole = numerator / (squared + detuning_ref[energy, band])
                folded = jnp.dot(rows, pole.astype(jnp.bfloat16), preferred_element_type=jnp.float32)
                out_ref[band, energy * states:(energy + 1) * states, columns] = folded.astype(jnp.bfloat16)
        return carry

    lax.fori_loop(0, amp_ref.shape[1] // inner, step, 0)


def fold(index, detuning_squared, rows, amp, freq, piece):
    stored, states, depth = rows.shape
    energies, bands = detuning_squared.shape
    width = tile_width(amp.shape[1], 1792)
    first, steps = piece
    cols = steps * width
    inner = tile_width(width, 896)
    return pl.pallas_call(
        functools.partial(fold_kernel, inner=inner),
        grid=(steps,),
        in_specs=[
            pl.BlockSpec(memory_space=pltpu.SMEM),
            pl.BlockSpec(memory_space=pltpu.SMEM),
            pl.BlockSpec((stored, states, depth), lambda i: (0, 0, 0)),
            pl.BlockSpec((depth, width), lambda i: (0, i + first)),
            pl.BlockSpec((depth, width), lambda i: (0, i + first)),
        ],
        out_specs=pl.BlockSpec((bands, energies * states, width), lambda i: (0, 0, i)),
        out_shape=jax.ShapeDtypeStruct((bands, energies * states, cols), jnp.bfloat16),
        compiler_params=pltpu.CompilerParams(vmem_limit_bytes=60 * 2**20),
        cost_estimate=pl.CostEstimate(
            flops=FOLD_FLOPS * cols // amp.shape[1], bytes_accessed=2 * depth * cols, transcendentals=0
        ),
        name="fold",
    )(index, detuning_squared, rows, amp, freq)


def pick_kernel(info_ref, mine_ref, other_ref, first_ref, second_ref, sems, *, base, at, me):
    held = mine_ref.shape[0]
    core = info_ref[me]
    for lane, out_ref in enumerate((first_ref, second_ref)):
        band = info_ref[at + base + lane]
        place = lax.rem(band, held)

        @pl.when(lax.div(band, held) == core)
        def _():
            pltpu.make_async_copy(mine_ref.at[place], out_ref, sems.at[lane]).start()

        @pl.when(lax.div(band, held) != core)
        def _():
            pltpu.make_async_copy(other_ref.at[place], out_ref, sems.at[lane]).start()

    for lane, out_ref in enumerate((first_ref, second_ref)):
        pltpu.make_async_copy(mine_ref.at[0], out_ref, sems.at[lane]).wait()


def pick(info, mine, other, base, at, me):
    shape = jax.ShapeDtypeStruct(mine.shape[1:], mine.dtype)
    return pl.pallas_call(
        functools.partial(pick_kernel, base=base, at=at, me=me),
        in_specs=[
            pl.BlockSpec(memory_space=pltpu.SMEM),
            pl.BlockSpec(memory_space=pltpu.HBM),
            pl.BlockSpec(memory_space=pltpu.HBM),
        ],
        out_specs=[pl.BlockSpec(memory_space=pltpu.VMEM)] * 2,
        out_shape=[shape, shape],
        scratch_shapes=[pltpu.SemaphoreType.DMA((2,))],
        compiler_params=pltpu.CompilerParams(vmem_limit_bytes=60 * 2**20),
        name="pick",
    )(info, mine, other)


def close_kernel(info_ref, *refs, window, pieces, reach, unit, base, at, me):
    halves = refs[:pieces]
    sources = refs[pieces:pieces + 2 + 4 * reach]
    out_ref, half_buf, column_buf, half_sems, column_sems = refs[pieces + 2 + 4 * reach:]
    core = info_ref[me]
    place = info_ref[me + 1]
    sign = 1 - 2 * core
    for band in range(window):
        apart = info_ref[band] - place
        lane = info_ref[window + band] - base
        for which in range(2):
            table = [(sources[which], 0)]
            for hop in range(1, reach + 1):
                table.append((sources[2 + 4 * (hop - 1) + which], sign * hop))
                table.append((sources[4 + 4 * (hop - 1) + which], -sign * hop))
            for ref, distance in table:
                @pl.when((lane == which) & (apart == distance))
                def _():
                    pltpu.make_async_copy(ref, column_buf.at[band], column_sems.at[band]).start()

    width = unit
    starts = []
    for half in halves:
        for part in range(half.shape[2] // width):
            place_in = pl.ds(part * width, width)
            pltpu.make_async_copy(half.at[:, :, place_in], half_buf.at[len(starts)], half_sems.at[len(starts)]).start()
            starts.append(part)
    for band in range(window):
        lane = info_ref[window + band] - base
        live = (lane >= 0) & (lane < 2)

        @pl.when(live)
        def _():
            pltpu.make_async_copy(sources[0], column_buf.at[band], column_sems.at[band]).wait()

        @pl.when(jnp.logical_not(live))
        def _():
            column_buf[band] = jnp.zeros_like(column_buf[band])

    def step(piece, total):
        pltpu.make_async_copy(halves[0].at[:, :, pl.ds(0, width)], half_buf.at[piece], half_sems.at[piece]).wait()
        columns = pl.ds(pl.multiple_of(piece * width, 128), width)
        for band in range(window):
            total += lax.dot_general(
                half_buf[piece, band], column_buf[band, :, columns], (((1,), (1,)), ((), ())),
                preferred_element_type=jnp.float32,
            )
        return total

    out_ref[...] = lax.fori_loop(0, len(starts), step, jnp.zeros(out_ref.shape, jnp.float32))


def close(info, halves, sources, reach, base, at, me):
    bands, pairs = halves[0].shape[:2]
    states, cols = sources[0].shape
    pieces = len(halves)
    unit = tile_width(cols, 1792)
    hbm = pl.BlockSpec(memory_space=pltpu.HBM)
    return pl.pallas_call(
        functools.partial(
            close_kernel, window=bands, pieces=pieces, reach=reach, unit=unit, base=base, at=at, me=me
        ),
        in_specs=[pl.BlockSpec(memory_space=pltpu.SMEM)] + [hbm] * (pieces + len(sources)),
        out_specs=pl.BlockSpec(memory_space=pltpu.VMEM),
        out_shape=jax.ShapeDtypeStruct((pairs, states), jnp.float32),
        scratch_shapes=[
            pltpu.VMEM((cols // unit, bands, pairs, unit), jnp.bfloat16),
            pltpu.VMEM((bands, states, cols), jnp.bfloat16),
            pltpu.SemaphoreType.DMA((cols // unit,)),
            pltpu.SemaphoreType.DMA((bands,)),
        ],
        compiler_params=pltpu.CompilerParams(vmem_limit_bytes=60 * 2**20),
        name="close",
    )(info, *halves, *sources)


def spread(lanes, n_ga):
    line = [(i + 1, i + 3) for i in range(0, n_ga - 2, 2)] + [(i + 2, i) for i in range(0, n_ga - 2, 2)]
    lanes = list(lanes)
    sources = list(lanes)
    for _ in range(1, n_ga // 2):
        hopped = []
        for lane in lanes:
            hopped.append(lax.ppermute(lane, "ga", line))
        lanes = hopped
        sources += lanes
        sources += [flip(lane, "ga", n_ga, 1) for lane in lanes]
    return sources


def row_pieces(matel, lanes, my_row, my_col, depth, n_ga, n_gp):
    held, states, cols = matel.shape
    local = min(cols, n_ga * depth)
    per_block = cols // depth
    pieces = matel[:, :, :local].reshape(held, states, local // depth, depth)
    pieces = jnp.moveaxis(pieces, 2, 0)
    if local < n_ga * depth:
        spare = jnp.zeros((n_ga - local // depth,) + pieces.shape[1:], pieces.dtype)
        pieces = jnp.concatenate([pieces, spare])
        pieces = jnp.roll(pieces, my_col * per_block, axis=0)
    pieces = pieces[:, None]
    bit = n_ga // 2
    while bit:
        upper = (my_row & bit) != 0
        half = pieces.shape[0] // 2
        keep = jnp.where(upper, pieces[half:], pieces[:half])
        send = jnp.where(upper, pieces[:half], pieces[half:])
        got = flip(send, "ga", n_ga, bit)
        pieces = jnp.where(
            upper, jnp.concatenate([got, keep], axis=1), jnp.concatenate([keep, got], axis=1)
        )
        if bit == n_ga // 2:
            pieces, lanes = lax.optimization_barrier((pieces, lanes))
        bit //= 2
    bits = n_ga.bit_length() - 1
    order = pieces[0].reshape((2,) * bits + pieces.shape[2:])
    order = jnp.transpose(order, tuple(reversed(range(bits))) + tuple(range(bits, order.ndim)))
    order = order.reshape((n_ga * held, states, depth))
    here = my_col == (my_row * depth) // cols
    rows = jnp.where(here, order, jnp.zeros((), matel.dtype))
    bit = 1
    while bit < n_gp:
        rows = rows + flip(rows, "gp", n_gp, bit)
        bit *= 2
    return rows, lanes


def shards(matel, pole_amp, pole_freq, band_energy, energies, owner, slot, *, n_ga, n_gp):
    held, states, cols = matel.shape
    depth = pole_amp.shape[0]
    window = owner.shape[0]
    my_row = lax.axis_index("ga")
    my_col = lax.axis_index("gp")
    other = flip(matel, "ga", n_ga, 1)

    chip = owner // 2
    number = (owner % 2) * held + slot
    numbers = jnp.arange(2 * held, dtype=jnp.int32)
    wanted = jnp.any(
        (chip[:, None, None] == chip[None, :, None]) & (number[None, :, None] == numbers), axis=1
    )
    rank = jnp.sum(wanted & (numbers < number[:, None]), axis=1, dtype=jnp.int32)
    on_mine = chip == my_row // 2
    picks = jnp.max(
        jnp.where(on_mine[:, None] & (rank[:, None] == numbers), number[:, None], 0), axis=0
    )
    info = jnp.concatenate([chip, rank, picks, (my_row % 2)[None], (my_row // 2)[None]]).astype(jnp.int32)
    at = 2 * window
    me = at + 2 * held

    index = owner * held + slot
    rows, lanes = row_pieces(matel, pick(info, matel, other, 0, at, me), my_row, my_col, depth, n_ga, n_gp)
    sources = spread(lanes, n_ga)
    labels = jnp.arange(n_ga * held, dtype=jnp.int32)
    level = jnp.sum(jnp.where(labels[None, :] == index[:, None], band_energy[None, :], 0.0), axis=1)
    detuning = energies[:, None] - level[None, :]
    blocks = cols // tile_width(cols, 1792)
    early = max(1, blocks // 7)
    middle = (blocks - early) // 2
    halves = []
    for number, piece in enumerate(((0, early), (early, middle), (early + middle, blocks - early - middle))):
        halves.append(fold(index, detuning * detuning, rows, pole_amp, pole_freq, piece))
    reach = n_ga // 2 - 1
    total = close(info, halves, sources, reach, 0, at, me)
    for more in range(1, held):
        def further(total):
            sources = spread(pick(info, matel, other, 2 * more, at, me), n_ga)
            return total + close(info, halves, sources, reach, 2 * more, at, me)

        total = lax.cond(jnp.max(rank) >= 2 * more, further, lambda total: total, total)

    total = gather_sum(total, "ga", n_ga, 1, 1)
    total = gather_sum(total, "ga", n_ga, 2, n_ga)
    total = gather_sum(total, "gp", n_gp, 1, n_gp)
    return total.reshape(energies.shape[0], states, states)


def solution(mesh):
    n_ga, n_gp = mesh.shape["ga"], mesh.shape["gp"]

    def body(*values):
        return shards(*values, n_ga=n_ga, n_gp=n_gp)

    return jax.shard_map(
        body,
        mesh=mesh,
        in_specs=(P("ga", None, "gp"), P("ga", "gp"), P("ga", "gp"), P(), P(), P(), P()),
        out_specs=P(),
        check_vma=False,
    )
```

profile of v0, /device:TPU:0, one launch (start us, length us, event | category | flops | bytes accessed | tf_op | source)
XLA Modules:
  0.0 128.2 jit_solution(8562105639717135753)
XLA Ops:
  1.4 3.7 %collective-permute-start.12 = (bf16[4,1,2,16,128]{4,0,3,2,1:T(4,128)(2,1)S(1)}, bf16[4,1,2,16,128]{4,0,3,2,1:T(4,128)(2,1)S(1)}, u32[]{:S(2)}, u32[]{:S(2)}) collective-permute-start(bf16[4,1,2,16,128]{4,0,3,2,1:T(4,128)(2,1)S(1)} %get-tuple-element.48), channel_id=1, source_target_pairs={{0,16},{4,20},{8,24},{12,28},{16,0},{20,4},{24,8},{28,12},{1,17},{... | collective-permute-start | bytes 98312 | tf_op jit(solution)/shard_map/ppermute | solution.py:15
  7.3 2.9 %pick.3 = (bf16[16,25088]{1,0:T(8,128)(2,1)}, bf16[16,25088]{1,0:T(8,128)(2,1)}) custom-call(s32[16]{0:T(128)S(1)} %concatenate.25.info_ref, bf16[2,16,25088]{2,1,0:T(8,128)(2,1)} %mine_ref.1, bf16[2,16,25088]{2,1,0:T(8,128)(2,1)S(1)} %collective-permute-done.13.other_ref), custom_call_target="tpu_custom_call" | custom-call | tf_op jit(solution)/shard_map/pick/pallas_call | solution.py:107
  10.2 1.3 %collective-permute-start.18 = (bf16[16,25088]{1,0:T(8,128)(2,1)}, bf16[16,25088]{1,0:T(8,128)(2,1)S(1)}, u32[]{:S(2)}, u32[]{:S(2)}) collective-permute-start(bf16[16,25088]{1,0:T(8,128)(2,1)} %get-tuple-element.40.refs_3_), channel_id=1, source_target_pairs={{4,12},{12,20},{20,28},{8,0},{16,8},{24,16},{5,13},{13,21},{21,29}... | collective-permute-start | bytes 2408456 | tf_op jit(solution)/shard_map/ppermute | solution.py:205
  12.9 3.3 %collective-permute-start.14 = (bf16[2,2,2,16,128]{4,0,3,2,1:T(2,128)(2,1)S(1)}, bf16[2,2,2,16,128]{4,0,3,2,1:T(2,128)(2,1)S(1)}, u32[]{:S(2)}, u32[]{:S(2)}) collective-permute-start(bf16[2,2,2,16,128]{4,0,3,2,1:T(2,128)(2,1)S(1)} %get-tuple-element.46), channel_id=1, source_target_pairs={{0,8},{4,12},{8,0},{12,4},{16,24},{20,28},{24,16},{28,20},{1,9},{5... | collective-permute-start | bytes 98312 | tf_op jit(solution)/shard_map/ppermute | solution.py:15
  16.3 17.5 %collective-permute-done.14 = bf16[2,2,2,16,128]{4,0,3,2,1:T(2,128)(2,1)S(1)} collective-permute-done((bf16[2,2,2,16,128]{4,0,3,2,1:T(2,128)(2,1)S(1)}, bf16[2,2,2,16,128]{4,0,3,2,1:T(2,128)(2,1)S(1)}, u32[]{:S(2)}, u32[]{:S(2)}) %collective-permute-start.14) | collective-permute-done | bytes 32800 | tf_op jit(solution)/shard_map/ppermute | solution.py:15
  35.3 1.3 %collective-permute-start.23 = (bf16[16,25088]{1,0:T(8,128)(2,1)}, bf16[16,25088]{1,0:T(8,128)(2,1)}, u32[]{:S(2)}, u32[]{:S(2)}) collective-permute-start(bf16[16,25088]{1,0:T(8,128)(2,1)} %collective-permute-done.19.refs_6_), channel_id=1, source_target_pairs={{4,12},{12,20},{20,28},{8,0},{16,8},{24,16},{5,13},{13,21},{21,29}... | collective-permute-start | bytes 2408456 | tf_op jit(solution)/shard_map/ppermute | solution.py:205
  36.8 3.6 %collective-permute-start.15 = (bf16[1,4,2,16,128]{4,0,3,2,1:T(2,128)(2,1)S(1)}, bf16[1,4,2,16,128]{4,0,3,2,1:T(2,128)(2,1)S(1)}, u32[]{:S(2)}, u32[]{:S(2)}) collective-permute-start(bf16[1,4,2,16,128]{4,0,3,2,1:T(2,128)(2,1)S(1)} %get-tuple-element.44), channel_id=1, source_target_pairs={{0,4},{4,0},{8,12},{12,8},{16,20},{20,16},{24,28},{28,24},{1,5},{5... | collective-permute-start | bytes 98312 | tf_op jit(solution)/shard_map/ppermute | solution.py:15
  41.6 1.6 %collective-permute-start.16 = (bf16[16,16,128]{2,1,0:T(8,128)(2,1)S(1)}, bf16[16,16,128]{2,1,0:T(8,128)(2,1)S(1)}, u32[]{:S(2)}, u32[]{:S(2)}) collective-permute-start(bf16[16,16,128]{2,1,0:T(8,128)(2,1)S(1)} %bitcast.20), channel_id=1, source_target_pairs={{0,1},{1,0},{2,3},{3,2},{4,5},{5,4},{6,7},{7,6},{8,9},{9,8},{10,11... | collective-permute-start | bytes 196616 | tf_op jit(solution)/shard_map/ppermute | solution.py:15
  44.0 2.0 %collective-permute-done.16 = bf16[16,16,128]{2,1,0:T(8,128)(2,1)S(1)} collective-permute-done((bf16[16,16,128]{2,1,0:T(8,128)(2,1)S(1)}, bf16[16,16,128]{2,1,0:T(8,128)(2,1)S(1)}, u32[]{:S(2)}, u32[]{:S(2)}) %collective-permute-start.16) | collective-permute-done | bytes 65568 | tf_op jit(solution)/shard_map/ppermute | solution.py:15
  46.1 1.6 %collective-permute-start.17 = (bf16[16,16,128]{2,1,0:T(8,128)(2,1)S(1)}, bf16[16,16,128]{2,1,0:T(8,128)(2,1)S(1)}, u32[]{:S(2)}, u32[]{:S(2)}) collective-permute-start(bf16[16,16,128]{2,1,0:T(8,128)(2,1)S(1)} %bitcast_add_fusion), channel_id=1, source_target_pairs={{0,2},{1,3},{2,0},{3,1},{4,6},{5,7},{6,4},{7,5},{8,10},{9,11},{10,... | collective-permute-start | bytes 196616 | tf_op jit(solution)/shard_map/ppermute | solution.py:15
  52.3 4.4 %collective-permute-done.23.refs_10_ = bf16[16,25088]{1,0:T(8,128)(2,1)} collective-permute-done((bf16[16,25088]{1,0:T(8,128)(2,1)}, bf16[16,25088]{1,0:T(8,128)(2,1)}, u32[]{:S(2)}, u32[]{:S(2)}) %collective-permute-start.23) | collective-permute-done | bytes 802848 | tf_op jit(solution)/shard_map/ppermute | solution.py:205
  58.0 15.1 %fold.4.refs_1_ = bf16[5,48,10752]{2,1,0:T(8,128)(2,1)} custom-call(s32[5]{0:T(128)} %copy-done.19, f32[3,5]{1,0:T(4,128)} %subtract_multiply_fusion.detuning_ref, bf16[16,16,128]{2,1,0:T(8,128)(2,1)} %add.54.rows_ref, bf16[128,25088]{1,0:T(8,128)(2,1)} %amp_ref.5, bf16[128,25088]{1,0:T(8,128)(2,1)} %freq_ref.5), custom_call_target="tpu_custom_call" | custom-call | flops 20571428864 | bytes 2752512 | tf_op jit(solution)/shard_map/fold/pallas_call | solution.py:66
  74.6 15.0 %fold.5.refs_2_ = bf16[5,48,10752]{2,1,0:T(8,128)(2,1)} custom-call(s32[5]{0:T(128)} %copy-done.19, f32[3,5]{1,0:T(4,128)} %subtract_multiply_fusion.detuning_ref, bf16[16,16,128]{2,1,0:T(8,128)(2,1)} %add.54.rows_ref, bf16[128,25088]{1,0:T(8,128)(2,1)} %amp_ref.5, bf16[128,25088]{1,0:T(8,128)(2,1)} %freq_ref.5), custom_call_target="tpu_custom_call" | custom-call | flops 20571428864 | bytes 2752512 | tf_op jit(solution)/shard_map/fold/pallas_call | solution.py:66
  89.7 5.6 %fold.3.refs_0_ = bf16[5,48,3584]{2,1,0:T(8,128)(2,1)S(1)} custom-call(s32[5]{0:T(128)} %copy-done.19, f32[3,5]{1,0:T(4,128)} %subtract_multiply_fusion.detuning_ref, bf16[16,16,128]{2,1,0:T(8,128)(2,1)} %add.54.rows_ref, bf16[128,25088]{1,0:T(8,128)(2,1)} %amp_ref.5, bf16[128,25088]{1,0:T(8,128)(2,1)} %freq_ref.5), custom_call_target="tpu_custom_call" | custom-call | flops 6857142784 | bytes 917504 | tf_op jit(solution)/shard_map/fold/pallas_call | solution.py:66
  96.2 9.6 %close.3 = f32[48,16]{1,0:T(8,128)} custom-call(s32[16]{0:T(128)} %copy-done.17, bf16[5,48,3584]{2,1,0:T(8,128)(2,1)S(1)} %fold.3.refs_0_, bf16[5,48,10752]{2,1,0:T(8,128)(2,1)} %fold.4.refs_1_, bf16[5,48,10752]{2,1,0:T(8,128)(2,1)} %fold.5.refs_2_, bf16[16,25088]{1,0:T(8,128)(2,1)} %get-tuple-element.40.refs_3_, ...), custom_call_target="tpu_custom_call" | custom-call | tf_op jit(solution)/shard_map/close/pallas_call | solution.py:180
  105.9 1.4 %collective-permute-done.30 = f32[48,16]{1,0:T(8,128)S(1)} collective-permute-done((f32[48,16]{1,0:T(8,128)}, f32[48,16]{1,0:T(8,128)S(1)}, u32[]{:S(2)}, u32[]{:S(2)}) %collective-permute-start.30) | collective-permute-done | bytes 3104 | tf_op jit(solution)/shard_map/ppermute | solution.py:15
  108.1 2.2 %collective-permute-start.31 = (f32[48,16]{1,0:T(8,128)S(1)}, f32[48,16]{1,0:T(8,128)S(1)}, u32[]{:S(2)}, u32[]{:S(2)}) collective-permute-start(f32[48,16]{1,0:T(8,128)S(1)} %add.55), channel_id=1, source_target_pairs={{0,8},{4,12},{8,0},{12,4},{16,24},{20,28},{24,16},{28,20},{1,9},{5... | collective-permute-start | bytes 9224 | tf_op jit(solution)/shard_map/ppermute | solution.py:15
  110.2 4.0 %collective-permute-start.32 = (f32[48,16]{1,0:T(8,128)S(1)}, f32[48,16]{1,0:T(8,128)S(1)}, u32[]{:S(2)}, u32[]{:S(2)}) collective-permute-start(f32[48,16]{1,0:T(8,128)S(1)} %add.55), channel_id=1, source_target_pairs={{0,16},{4,20},{8,24},{12,28},{16,0},{20,4},{24,8},{28,12},{1,17},{... | collective-permute-start | bytes 9224 | tf_op jit(solution)/shard_map/ppermute | solution.py:15
  114.2 1.9 %collective-permute-done.32 = f32[48,16]{1,0:T(8,128)S(1)} collective-permute-done((f32[48,16]{1,0:T(8,128)S(1)}, f32[48,16]{1,0:T(8,128)S(1)}, u32[]{:S(2)}, u32[]{:S(2)}) %collective-permute-start.32) | collective-permute-done | bytes 3104 | tf_op jit(solution)/shard_map/ppermute | solution.py:15
  116.2 3.7 %collective-permute-done.33 = f32[48,16]{1,0:T(8,128)S(1)} collective-permute-done((f32[48,16]{1,0:T(8,128)S(1)}, f32[48,16]{1,0:T(8,128)S(1)}, u32[]{:S(2)}, u32[]{:S(2)}) %collective-permute-start.33) | collective-permute-done | bytes 3104 | tf_op jit(solution)/shard_map/ppermute | solution.py:15
  119.9 1.6 %collective-permute-start.34 = (f32[48,16]{1,0:T(8,128)S(1)}, f32[48,16]{1,0:T(8,128)S(1)}, u32[]{:S(2)}, u32[]{:S(2)}) collective-permute-start(f32[48,16]{1,0:T(8,128)S(1)} %add_add_fusion.1), channel_id=1, source_target_pairs={{0,1},{1,0},{2,3},{3,2},{4,5},{5,4},{6,7},{7,6},{8,9},{9,8},{10,11... | collective-permute-start | bytes 9224 | tf_op jit(solution)/shard_map/ppermute | solution.py:15
  121.4 1.5 %collective-permute-start.35 = (f32[48,16]{1,0:T(8,128)S(1)}, f32[48,16]{1,0:T(8,128)S(1)}, u32[]{:S(2)}, u32[]{:S(2)}) collective-permute-start(f32[48,16]{1,0:T(8,128)S(1)} %add_add_fusion.1), channel_id=1, source_target_pairs={{0,2},{1,3},{2,0},{3,1},{4,6},{5,7},{6,4},{7,5},{8,10},{9,11},{10,... | collective-permute-start | bytes 9224 | tf_op jit(solution)/shard_map/ppermute | solution.py:15
  124.0 1.3 %collective-permute-done.35 = f32[48,16]{1,0:T(8,128)S(1)} collective-permute-done((f32[48,16]{1,0:T(8,128)S(1)}, f32[48,16]{1,0:T(8,128)S(1)}, u32[]{:S(2)}, u32[]{:S(2)}) %collective-permute-start.35) | collective-permute-done | bytes 3104 | tf_op jit(solution)/shard_map/ppermute | solution.py:15
  125.3 2.4 %collective-permute-done.36 = f32[48,16]{1,0:T(8,128)S(1)} collective-permute-done((f32[48,16]{1,0:T(8,128)S(1)}, f32[48,16]{1,0:T(8,128)S(1)}, u32[]{:S(2)}, u32[]{:S(2)}) %collective-permute-start.36) | collective-permute-done | bytes 3104 | tf_op jit(solution)/shard_map/ppermute | solution.py:15
  (76 shorter events, 19.0 us)
Async XLA Ops:
  0.0 7.3 %collective-permute-start.13 = (bf16[2,16,25088]{2,1,0:T(8,128)(2,1)}, bf16[2,16,25088]{2,1,0:T(8,128)(2,1)S(1)}, u32[]{:S(2)}, u32[]{:S(2)}) collective-permute-start(bf16[2,16,25088]{2,1,0:T(8,128)(2,1)} %mine_ref.1), channel_id=1, source_target_pairs={{0,4},{4,0},{8,12},{12,8},{16,20},{20,16},{24,28},{28,24},{1,5},{5... | collective-permute-start | bytes 4816904 | tf_op jit(solution)/shard_map/ppermute | solution.py:15
  1.4 5.8 %collective-permute-start.12 = (bf16[4,1,2,16,128]{4,0,3,2,1:T(4,128)(2,1)S(1)}, bf16[4,1,2,16,128]{4,0,3,2,1:T(4,128)(2,1)S(1)}, u32[]{:S(2)}, u32[]{:S(2)}) collective-permute-start(bf16[4,1,2,16,128]{4,0,3,2,1:T(4,128)(2,1)S(1)} %get-tuple-element.48), channel_id=1, source_target_pairs={{0,16},{4,20},{8,24},{12,28},{16,0},{20,4},{24,8},{28,12},{1,17},{... | collective-permute-start | bytes 98312 | tf_op jit(solution)/shard_map/ppermute | solution.py:15
  10.2 23.7 %collective-permute-start.18 = (bf16[16,25088]{1,0:T(8,128)(2,1)}, bf16[16,25088]{1,0:T(8,128)(2,1)S(1)}, u32[]{:S(2)}, u32[]{:S(2)}) collective-permute-start(bf16[16,25088]{1,0:T(8,128)(2,1)} %get-tuple-element.40.refs_3_), channel_id=1, source_target_pairs={{4,12},{12,20},{20,28},{8,0},{16,8},{24,16},{5,13},{13,21},{21,29}... | collective-permute-start | bytes 2408456 | tf_op jit(solution)/shard_map/ppermute | solution.py:205
  11.5 23.8 %collective-permute-start.19 = (bf16[16,25088]{1,0:T(8,128)(2,1)}, bf16[16,25088]{1,0:T(8,128)(2,1)}, u32[]{:S(2)}, u32[]{:S(2)}) collective-permute-start(bf16[16,25088]{1,0:T(8,128)(2,1)} %get-tuple-element.41.refs_4_), channel_id=1, source_target_pairs={{4,12},{12,20},{20,28},{8,0},{16,8},{24,16},{5,13},{13,21},{21,29}... | collective-permute-start | bytes 2408456 | tf_op jit(solution)/shard_map/ppermute | solution.py:205
  12.9 20.9 %collective-permute-start.14 = (bf16[2,2,2,16,128]{4,0,3,2,1:T(2,128)(2,1)S(1)}, bf16[2,2,2,16,128]{4,0,3,2,1:T(2,128)(2,1)S(1)}, u32[]{:S(2)}, u32[]{:S(2)}) collective-permute-start(bf16[2,2,2,16,128]{4,0,3,2,1:T(2,128)(2,1)S(1)} %get-tuple-element.46), channel_id=1, source_target_pairs={{0,8},{4,12},{8,0},{12,4},{16,24},{20,28},{24,16},{28,20},{1,9},{5... | collective-permute-start | bytes 98312 | tf_op jit(solution)/shard_map/ppermute | solution.py:15
  34.0 17.1 %collective-permute-start.22 = (bf16[16,25088]{1,0:T(8,128)(2,1)S(1)}, bf16[16,25088]{1,0:T(8,128)(2,1)}, u32[]{:S(2)}, u32[]{:S(2)}) collective-permute-start(bf16[16,25088]{1,0:T(8,128)(2,1)S(1)} %collective-permute-done.18.refs_5_), channel_id=1, source_target_pairs={{4,12},{12,20},{20,28},{8,0},{16,8},{24,16},{5,13},{13,21},{21,29}... | collective-permute-start | bytes 2408456 | tf_op jit(solution)/shard_map/ppermute | solution.py:205
  35.3 21.4 %collective-permute-start.23 = (bf16[16,25088]{1,0:T(8,128)(2,1)}, bf16[16,25088]{1,0:T(8,128)(2,1)}, u32[]{:S(2)}, u32[]{:S(2)}) collective-permute-start(bf16[16,25088]{1,0:T(8,128)(2,1)} %collective-permute-done.19.refs_6_), channel_id=1, source_target_pairs={{4,12},{12,20},{20,28},{8,0},{16,8},{24,16},{5,13},{13,21},{21,29}... | collective-permute-start | bytes 2408456 | tf_op jit(solution)/shard_map/ppermute | solution.py:205
  36.8 4.5 %collective-permute-start.15 = (bf16[1,4,2,16,128]{4,0,3,2,1:T(2,128)(2,1)S(1)}, bf16[1,4,2,16,128]{4,0,3,2,1:T(2,128)(2,1)S(1)}, u32[]{:S(2)}, u32[]{:S(2)}) collective-permute-start(bf16[1,4,2,16,128]{4,0,3,2,1:T(2,128)(2,1)S(1)} %get-tuple-element.44), channel_id=1, source_target_pairs={{0,4},{4,0},{8,12},{12,8},{16,20},{20,16},{24,28},{28,24},{1,5},{5... | collective-permute-start | bytes 98312 | tf_op jit(solution)/shard_map/ppermute | solution.py:15
  41.6 4.4 %collective-permute-start.16 = (bf16[16,16,128]{2,1,0:T(8,128)(2,1)S(1)}, bf16[16,16,128]{2,1,0:T(8,128)(2,1)S(1)}, u32[]{:S(2)}, u32[]{:S(2)}) collective-permute-start(bf16[16,16,128]{2,1,0:T(8,128)(2,1)S(1)} %bitcast.20), channel_id=1, source_target_pairs={{0,1},{1,0},{2,3},{3,2},{4,5},{5,4},{6,7},{7,6},{8,9},{9,8},{10,11... | collective-permute-start | bytes 196616 | tf_op jit(solution)/shard_map/ppermute | solution.py:15
  46.1 4.3 %collective-permute-start.17 = (bf16[16,16,128]{2,1,0:T(8,128)(2,1)S(1)}, bf16[16,16,128]{2,1,0:T(8,128)(2,1)S(1)}, u32[]{:S(2)}, u32[]{:S(2)}) collective-permute-start(bf16[16,16,128]{2,1,0:T(8,128)(2,1)S(1)} %bitcast_add_fusion), channel_id=1, source_target_pairs={{0,2},{1,3},{2,0},{3,1},{4,6},{5,7},{6,4},{7,5},{8,10},{9,11},{10,... | collective-permute-start | bytes 196616 | tf_op jit(solution)/shard_map/ppermute | solution.py:15
  51.0 22.7 %collective-permute-start.20 = (bf16[16,25088]{1,0:T(8,128)(2,1)S(1)}, bf16[16,25088]{1,0:T(8,128)(2,1)S(1)}, u32[]{:S(2)}, u32[]{:S(2)}) collective-permute-start(bf16[16,25088]{1,0:T(8,128)(2,1)S(1)} %collective-permute-done.18.refs_5_), channel_id=1, source_target_pairs={{0,4},{4,0},{8,12},{12,8},{16,20},{20,16},{24,28},{28,24},{1,5},{5... | collective-permute-start | bytes 2408456 | tf_op jit(solution)/shard_map/ppermute | solution.py:15
  51.0 23.1 %collective-permute-start.26 = (bf16[16,25088]{1,0:T(8,128)(2,1)}, bf16[16,25088]{1,0:T(8,128)(2,1)}, u32[]{:S(2)}, u32[]{:S(2)}) collective-permute-start(bf16[16,25088]{1,0:T(8,128)(2,1)} %collective-permute-done.22.refs_9_), channel_id=1, source_target_pairs={{4,12},{12,20},{20,28},{8,0},{16,8},{24,16},{5,13},{13,21},{21,29}... | collective-permute-start | bytes 2408456 | tf_op jit(solution)/shard_map/ppermute | solution.py:205
  56.7 17.5 %collective-permute-start.27 = (bf16[16,25088]{1,0:T(8,128)(2,1)}, bf16[16,25088]{1,0:T(8,128)(2,1)}, u32[]{:S(2)}, u32[]{:S(2)}) collective-permute-start(bf16[16,25088]{1,0:T(8,128)(2,1)} %collective-permute-done.23.refs_10_), channel_id=1, source_target_pairs={{4,12},{12,20},{20,28},{8,0},{16,8},{24,16},{5,13},{13,21},{21,29}... | collective-permute-start | bytes 2408456 | tf_op jit(solution)/shard_map/ppermute | solution.py:205
  73.1 22.2 %collective-permute-start.21 = (bf16[16,25088]{1,0:T(8,128)(2,1)}, bf16[16,25088]{1,0:T(8,128)(2,1)}, u32[]{:S(2)}, u32[]{:S(2)}) collective-permute-start(bf16[16,25088]{1,0:T(8,128)(2,1)} %collective-permute-done.19.refs_6_), channel_id=1, source_target_pairs={{0,4},{4,0},{8,12},{12,8},{16,20},{20,16},{24,28},{28,24},{1,5},{5... | collective-permute-start | bytes 2408456 | tf_op jit(solution)/shard_map/ppermute | solution.py:15
  73.6 21.7 %collective-permute-start.24 = (bf16[16,25088]{1,0:T(8,128)(2,1)}, bf16[16,25088]{1,0:T(8,128)(2,1)}, u32[]{:S(2)}, u32[]{:S(2)}) collective-permute-start(bf16[16,25088]{1,0:T(8,128)(2,1)} %collective-permute-done.22.refs_9_), channel_id=1, source_target_pairs={{0,4},{4,0},{8,12},{12,8},{16,20},{20,16},{24,28},{28,24},{1,5},{5... | collective-permute-start | bytes 2408456 | tf_op jit(solution)/shard_map/ppermute | solution.py:15
  73.7 21.6 %collective-permute-start.25 = (bf16[16,25088]{1,0:T(8,128)(2,1)}, bf16[16,25088]{1,0:T(8,128)(2,1)S(1)}, u32[]{:S(2)}, u32[]{:S(2)}) collective-permute-start(bf16[16,25088]{1,0:T(8,128)(2,1)} %collective-permute-done.23.refs_10_), channel_id=1, source_target_pairs={{0,4},{4,0},{8,12},{12,8},{16,20},{20,16},{24,28},{28,24},{1,5},{5... | collective-permute-start | bytes 2408456 | tf_op jit(solution)/shard_map/ppermute | solution.py:15
  74.1 21.2 %collective-permute-start.28 = (bf16[16,25088]{1,0:T(8,128)(2,1)}, bf16[16,25088]{1,0:T(8,128)(2,1)}, u32[]{:S(2)}, u32[]{:S(2)}) collective-permute-start(bf16[16,25088]{1,0:T(8,128)(2,1)} %collective-permute-done.26.refs_13_), channel_id=1, source_target_pairs={{0,4},{4,0},{8,12},{12,8},{16,20},{20,16},{24,28},{28,24},{1,5},{5... | collective-permute-start | bytes 2408456 | tf_op jit(solution)/shard_map/ppermute | solution.py:15
  74.2 21.1 %collective-permute-start.29 = (bf16[16,25088]{1,0:T(8,128)(2,1)}, bf16[16,25088]{1,0:T(8,128)(2,1)}, u32[]{:S(2)}, u32[]{:S(2)}) collective-permute-start(bf16[16,25088]{1,0:T(8,128)(2,1)} %collective-permute-done.27.refs_14_), channel_id=1, source_target_pairs={{0,4},{4,0},{8,12},{12,8},{16,20},{20,16},{24,28},{28,24},{1,5},{5... | collective-permute-start | bytes 2408456 | tf_op jit(solution)/shard_map/ppermute | solution.py:15
  108.1 6.2 %collective-permute-start.31 = (f32[48,16]{1,0:T(8,128)S(1)}, f32[48,16]{1,0:T(8,128)S(1)}, u32[]{:S(2)}, u32[]{:S(2)}) collective-permute-start(f32[48,16]{1,0:T(8,128)S(1)} %add.55), channel_id=1, source_target_pairs={{0,8},{4,12},{8,0},{12,4},{16,24},{20,28},{24,16},{28,20},{1,9},{5... | collective-permute-start | bytes 9224 | tf_op jit(solution)/shard_map/ppermute | solution.py:15
  110.2 5.9 %collective-permute-start.32 = (f32[48,16]{1,0:T(8,128)S(1)}, f32[48,16]{1,0:T(8,128)S(1)}, u32[]{:S(2)}, u32[]{:S(2)}) collective-permute-start(f32[48,16]{1,0:T(8,128)S(1)} %add.55), channel_id=1, source_target_pairs={{0,16},{4,20},{8,24},{12,28},{16,0},{20,4},{24,8},{28,12},{1,17},{... | collective-permute-start | bytes 9224 | tf_op jit(solution)/shard_map/ppermute | solution.py:15
  114.2 5.6 %collective-permute-start.33 = (f32[48,16]{1,0:T(8,128)S(1)}, f32[48,16]{1,0:T(8,128)S(1)}, u32[]{:S(2)}, u32[]{:S(2)}) collective-permute-start(f32[48,16]{1,0:T(8,128)S(1)} %add.55), channel_id=1, source_target_pairs={{0,24},{4,28},{8,16},{12,20},{16,8},{20,12},{24,0},{28,4},{1,25},{... | collective-permute-start | bytes 9224 | tf_op jit(solution)/shard_map/ppermute | solution.py:15
  119.9 4.1 %collective-permute-start.34 = (f32[48,16]{1,0:T(8,128)S(1)}, f32[48,16]{1,0:T(8,128)S(1)}, u32[]{:S(2)}, u32[]{:S(2)}) collective-permute-start(f32[48,16]{1,0:T(8,128)S(1)} %add_add_fusion.1), channel_id=1, source_target_pairs={{0,1},{1,0},{2,3},{3,2},{4,5},{5,4},{6,7},{7,6},{8,9},{9,8},{10,11... | collective-permute-start | bytes 9224 | tf_op jit(solution)/shard_map/ppermute | solution.py:15
  121.4 3.8 %collective-permute-start.35 = (f32[48,16]{1,0:T(8,128)S(1)}, f32[48,16]{1,0:T(8,128)S(1)}, u32[]{:S(2)}, u32[]{:S(2)}) collective-permute-start(f32[48,16]{1,0:T(8,128)S(1)} %add_add_fusion.1), channel_id=1, source_target_pairs={{0,2},{1,3},{2,0},{3,1},{4,6},{5,7},{6,4},{7,5},{8,10},{9,11},{10,... | collective-permute-start | bytes 9224 | tf_op jit(solution)/shard_map/ppermute | solution.py:15
  122.9 4.7 %collective-permute-start.36 = (f32[48,16]{1,0:T(8,128)S(1)}, f32[48,16]{1,0:T(8,128)S(1)}, u32[]{:S(2)}, u32[]{:S(2)}) collective-permute-start(f32[48,16]{1,0:T(8,128)S(1)} %add_add_fusion.1), channel_id=1, source_target_pairs={{0,3},{1,2},{2,1},{3,0},{4,7},{5,6},{6,5},{7,4},{8,11},{9,10},{10,... | collective-permute-start | bytes 9224 | tf_op jit(solution)/shard_map/ppermute | solution.py:15
  (9 other events, 261.7 us)
where the time goes:
time: 129 us; the launch traced here: 128 us
  Pallas kernels  48.2 us (37%)
  waiting for transfers between devices  37 us (29%)
  starting transfers between devices  33.3 us (26%)
  other arithmetic  6.87 us (5%)
  local copies, waits for them, and re-layouts  1.98 us (2%)
    pallas_call x3, Pallas kernels, fold(): pl.pallas_call(functools.partial(fold_kernel, inner=inner), grid=(steps,)...  35.7 us
    ppermute x19, waiting for transfers between devices, flip(): return lax.ppermute(values, axis, [(i, i ^ bit) for i in range(size)])  32.6 us
    ppermute x19, starting transfers between devices, flip(): return lax.ppermute(values, axis, [(i, i ^ bit) for i in range(size)])  25.5 us
    pallas_call x1, Pallas kernels, close(): pl.pallas_call(functools.partial(close_kernel, window=bands, pieces=piece...  9.56 us
    ppermute x6, starting transfers between devices, spread(): hopped.append(lax.ppermute(lane, 'ga', line))  7.73 us
    ppermute x6, waiting for transfers between devices, spread(): hopped.append(lax.ppermute(lane, 'ga', line))  4.43 us
    pallas_call x1, Pallas kernels, pick(): pl.pallas_call(functools.partial(pick_kernel, base=base, at=at, me=me), i...  2.88 us
  transfers between devices with their start and end apart: 25, of which 11 were waited for; matrix products, arithmetic and copies ran while one was open for 5% of the time, Pallas kernels for 28%

commit v1 on v0

--- a/solution.py
+++ b/solution.py
@@ -205,7 +205,8 @@
             hopped.append(lax.ppermute(lane, "ga", line))
         lanes = hopped
         sources += lanes
-        sources += [flip(lane, "ga", n_ga, 1) for lane in lanes]
+        for lane in lanes:
+            sources.append(flip(lane, "ga", n_ga, 1))
     return sources
 
 
@@ -230,7 +231,7 @@
         pieces = jnp.where(
             upper, jnp.concatenate([got, keep], axis=1), jnp.concatenate([keep, got], axis=1)
         )
-        if bit == n_ga // 2:
+        if bit == min(2, n_ga // 2):
             pieces, lanes = lax.optimization_barrier((pieces, lanes))
         bit //= 2
     bits = n_ga.bit_length() - 1

time: 129 us -> 127 us (0.984)
  starting transfers between devices: 33.3 us -> 29.6 us
  waiting for transfers between devices: 37 us -> 38.6 us
    ppermute x6, waiting for transfers between devices: 4.43 us -> 22.5 us  [spread(): hopped.append(lax.ppermute(lane, 'ga', line))]
    ppermute x19, waiting for transfers between devices: 32.6 us -> 16.1 us  [flip(): return lax.ppermute(values, axis, [(i, i ^ bit) for i in range(size)])]
    ppermute x19, starting transfers between devices: 25.5 us -> 21.9 us  [flip(): return lax.ppermute(values, axis, [(i, i ^ bit) for i in range(size)])]
  transfers between devices with their start and end apart: 25 -> 25, of which waited for: 11 -> 14; matrix products, arithmetic and copies ran while one was open for 5% -> 5% of each run, Pallas kernels for 28% -> 28%
where the time goes in v1:
time: 127 us; the launch traced here: 126 us
  Pallas kernels  48.2 us (38%)
  waiting for transfers between devices  38.6 us (30%)
  starting transfers between devices  29.6 us (23%)
  other arithmetic  6.87 us (5%)
  local copies, waits for them, and re-layouts  1.98 us (2%)
    pallas_call x3, Pallas kernels, fold(): pl.pallas_call(functools.partial(fold_kernel, inner=inner), grid=(steps,)...  35.7 us
    ppermute x6, waiting for transfers between devices, spread(): hopped.append(lax.ppermute(lane, 'ga', line))  22.5 us
    ppermute x19, starting transfers between devices, flip(): return lax.ppermute(values, axis, [(i, i ^ bit) for i in range(size)])  21.9 us
    ppermute x19, waiting for transfers between devices, flip(): return lax.ppermute(values, axis, [(i, i ^ bit) for i in range(size)])  16.1 us
    pallas_call x1, Pallas kernels, close(): pl.pallas_call(functools.partial(close_kernel, window=bands, pieces=piece...  9.56 us
    ppermute x6, starting transfers between devices, spread(): hopped.append(lax.ppermute(lane, 'ga', line))  7.71 us
    pallas_call x1, Pallas kernels, pick(): pl.pallas_call(functools.partial(pick_kernel, base=base, at=at, me=me), i...  2.88 us
  transfers between devices with their start and end apart: 25, of which 14 were waited for; matrix products, arithmetic and copies ran while one was open for 5% of the time, Pallas kernels for 28%

profile of v1, /device:TPU:0, one launch (start us, length us, event | category | flops | bytes accessed | tf_op | source)
XLA Modules:
  0.0 126.1 jit_solution(8799849262811237884)
XLA Ops:
  1.4 3.7 %collective-permute-start.12 = (bf16[4,1,2,16,128]{4,0,3,2,1:T(4,128)(2,1)S(1)}, bf16[4,1,2,16,128]{4,0,3,2,1:T(4,128)(2,1)S(1)}, u32[]{:S(2)}, u32[]{:S(2)}) collective-permute-start(bf16[4,1,2,16,128]{4,0,3,2,1:T(4,128)(2,1)S(1)} %get-tuple-element.48), channel_id=1, source_target_pairs={{0,16},{4,20},{8,24},{12,28},{16,0},{20,4},{24,8},{28,12},{1,17},{... | collective-permute-start | bytes 98312 | tf_op jit(solution)/shard_map/ppermute | solution.py:15
  7.3 1.8 %collective-permute-start.13 = (bf16[2,2,2,16,128]{4,0,3,2,1:T(2,128)(2,1)S(1)}, bf16[2,2,2,16,128]{4,0,3,2,1:T(2,128)(2,1)S(1)}, u32[]{:S(2)}, u32[]{:S(2)}) collective-permute-start(bf16[2,2,2,16,128]{4,0,3,2,1:T(2,128)(2,1)S(1)} %get-tuple-element.46), channel_id=1, source_target_pairs={{0,8},{4,12},{8,0},{12,4},{16,24},{20,28},{24,16},{28,20},{1,9},{5... | collective-permute-start | bytes 98312 | tf_op jit(solution)/shard_map/ppermute | solution.py:15
  9.3 2.0 %collective-permute-done.13 = bf16[2,2,2,16,128]{4,0,3,2,1:T(2,128)(2,1)S(1)} collective-permute-done((bf16[2,2,2,16,128]{4,0,3,2,1:T(2,128)(2,1)S(1)}, bf16[2,2,2,16,128]{4,0,3,2,1:T(2,128)(2,1)S(1)}, u32[]{:S(2)}, u32[]{:S(2)}) %collective-permute-start.13) | collective-permute-done | bytes 32800 | tf_op jit(solution)/shard_map/ppermute | solution.py:15
  11.4 2.9 %pick.3 = (bf16[16,25088]{1,0:T(8,128)(2,1)}, bf16[16,25088]{1,0:T(8,128)(2,1)}) custom-call(s32[16]{0:T(128)S(1)} %concatenate.25.info_ref, bf16[2,16,25088]{2,1,0:T(8,128)(2,1)} %mine_ref.1, bf16[2,16,25088]{2,1,0:T(8,128)(2,1)S(1)} %collective-permute-done.14.other_ref), custom_call_target="tpu_custom_call" | custom-call | tf_op jit(solution)/shard_map/pick/pallas_call | solution.py:107
  14.3 1.3 %collective-permute-start.18 = (bf16[16,25088]{1,0:T(8,128)(2,1)}, bf16[16,25088]{1,0:T(8,128)(2,1)S(1)}, u32[]{:S(2)}, u32[]{:S(2)}) collective-permute-start(bf16[16,25088]{1,0:T(8,128)(2,1)} %get-tuple-element.40.refs_3_), channel_id=1, source_target_pairs={{4,12},{12,20},{20,28},{8,0},{16,8},{24,16},{5,13},{13,21},{21,29}... | collective-permute-start | bytes 2408456 | tf_op jit(solution)/shard_map/ppermute | solution.py:205
  16.9 11.7 %collective-permute-done.18.refs_5_ = bf16[16,25088]{1,0:T(8,128)(2,1)S(1)} collective-permute-done((bf16[16,25088]{1,0:T(8,128)(2,1)}, bf16[16,25088]{1,0:T(8,128)(2,1)S(1)}, u32[]{:S(2)}, u32[]{:S(2)}) %collective-permute-start.18) | collective-permute-done | bytes 802848 | tf_op jit(solution)/shard_map/ppermute | solution.py:205
  29.9 7.4 %collective-permute-done.19.refs_6_ = bf16[16,25088]{1,0:T(8,128)(2,1)} collective-permute-done((bf16[16,25088]{1,0:T(8,128)(2,1)}, bf16[16,25088]{1,0:T(8,128)(2,1)}, u32[]{:S(2)}, u32[]{:S(2)}) %collective-permute-start.19) | collective-permute-done | bytes 802848 | tf_op jit(solution)/shard_map/ppermute | solution.py:205
  40.4 1.7 %collective-permute-start.16 = (bf16[16,16,128]{2,1,0:T(8,128)(2,1)S(1)}, bf16[16,16,128]{2,1,0:T(8,128)(2,1)S(1)}, u32[]{:S(2)}, u32[]{:S(2)}) collective-permute-start(bf16[16,16,128]{2,1,0:T(8,128)(2,1)S(1)} %bitcast.20), channel_id=1, source_target_pairs={{0,1},{1,0},{2,3},{3,2},{4,5},{5,4},{6,7},{7,6},{8,9},{9,8},{10,11... | collective-permute-start | bytes 196616 | tf_op jit(solution)/shard_map/ppermute | solution.py:15
  43.0 1.8 %collective-permute-done.16 = bf16[16,16,128]{2,1,0:T(8,128)(2,1)S(1)} collective-permute-done((bf16[16,16,128]{2,1,0:T(8,128)(2,1)S(1)}, bf16[16,16,128]{2,1,0:T(8,128)(2,1)S(1)}, u32[]{:S(2)}, u32[]{:S(2)}) %collective-permute-start.16) | collective-permute-done | bytes 65568 | tf_op jit(solution)/shard_map/ppermute | solution.py:15
  44.8 1.8 %collective-permute-start.17 = (bf16[16,16,128]{2,1,0:T(8,128)(2,1)S(1)}, bf16[16,16,128]{2,1,0:T(8,128)(2,1)S(1)}, u32[]{:S(2)}, u32[]{:S(2)}) collective-permute-start(bf16[16,16,128]{2,1,0:T(8,128)(2,1)S(1)} %bitcast_add_fusion), channel_id=1, source_target_pairs={{0,2},{1,3},{2,0},{3,1},{4,6},{5,7},{6,4},{7,5},{8,10},{9,11},{10,... | collective-permute-start | bytes 196616 | tf_op jit(solution)/shard_map/ppermute | solution.py:15
  51.0 3.5 %collective-permute-done.23.refs_10_ = bf16[16,25088]{1,0:T(8,128)(2,1)} collective-permute-done((bf16[16,25088]{1,0:T(8,128)(2,1)}, bf16[16,25088]{1,0:T(8,128)(2,1)}, u32[]{:S(2)}, u32[]{:S(2)}) %collective-permute-start.23) | collective-permute-done | bytes 802848 | tf_op jit(solution)/shard_map/ppermute | solution.py:205
  55.8 15.1 %fold.4.refs_1_ = bf16[5,48,10752]{2,1,0:T(8,128)(2,1)} custom-call(s32[5]{0:T(128)} %copy-done.19, f32[3,5]{1,0:T(4,128)} %subtract_multiply_fusion.detuning_ref, bf16[16,16,128]{2,1,0:T(8,128)(2,1)} %add.54.rows_ref, bf16[128,25088]{1,0:T(8,128)(2,1)} %amp_ref.5, bf16[128,25088]{1,0:T(8,128)(2,1)} %freq_ref.5), custom_call_target="tpu_custom_call" | custom-call | flops 20571428864 | bytes 2752512 | tf_op jit(solution)/shard_map/fold/pallas_call | solution.py:66
  70.9 3.3 %collective-permute-start.21 = (bf16[16,25088]{1,0:T(8,128)(2,1)}, bf16[16,25088]{1,0:T(8,128)(2,1)}, u32[]{:S(2)}, u32[]{:S(2)}) collective-permute-start(bf16[16,25088]{1,0:T(8,128)(2,1)} %collective-permute-done.19.refs_6_), channel_id=1, source_target_pairs={{0,4},{4,0},{8,12},{12,8},{16,20},{20,16},{24,28},{28,24},{1,5},{5... | collective-permute-start | bytes 2408456 | tf_op jit(solution)/shard_map/ppermute | solution.py:15
  75.2 15.0 %fold.5.refs_2_ = bf16[5,48,10752]{2,1,0:T(8,128)(2,1)} custom-call(s32[5]{0:T(128)} %copy-done.19, f32[3,5]{1,0:T(4,128)} %subtract_multiply_fusion.detuning_ref, bf16[16,16,128]{2,1,0:T(8,128)(2,1)} %add.54.rows_ref, bf16[128,25088]{1,0:T(8,128)(2,1)} %amp_ref.5, bf16[128,25088]{1,0:T(8,128)(2,1)} %freq_ref.5), custom_call_target="tpu_custom_call" | custom-call | flops 20571428864 | bytes 2752512 | tf_op jit(solution)/shard_map/fold/pallas_call | solution.py:66
  90.3 5.6 %fold.3.refs_0_ = bf16[5,48,3584]{2,1,0:T(8,128)(2,1)S(1)} custom-call(s32[5]{0:T(128)} %copy-done.19, f32[3,5]{1,0:T(4,128)} %subtract_multiply_fusion.detuning_ref, bf16[16,16,128]{2,1,0:T(8,128)(2,1)} %add.54.rows_ref, bf16[128,25088]{1,0:T(8,128)(2,1)} %amp_ref.5, bf16[128,25088]{1,0:T(8,128)(2,1)} %freq_ref.5), custom_call_target="tpu_custom_call" | custom-call | flops 6857142784 | bytes 917504 | tf_op jit(solution)/shard_map/fold/pallas_call | solution.py:66
  96.8 9.6 %close.3 = f32[48,16]{1,0:T(8,128)} custom-call(s32[16]{0:T(128)} %copy-done.17, bf16[5,48,3584]{2,1,0:T(8,128)(2,1)S(1)} %fold.3.refs_0_, bf16[5,48,10752]{2,1,0:T(8,128)(2,1)} %fold.4.refs_1_, bf16[5,48,10752]{2,1,0:T(8,128)(2,1)} %fold.5.refs_2_, bf16[16,25088]{1,0:T(8,128)(2,1)} %get-tuple-element.40.refs_3_, ...), custom_call_target="tpu_custom_call" | custom-call | tf_op jit(solution)/shard_map/close/pallas_call | solution.py:180
  106.5 1.4 %collective-permute-done.30 = f32[48,16]{1,0:T(8,128)S(1)} collective-permute-done((f32[48,16]{1,0:T(8,128)}, f32[48,16]{1,0:T(8,128)S(1)}, u32[]{:S(2)}, u32[]{:S(2)}) %collective-permute-start.30) | collective-permute-done | bytes 3104 | tf_op jit(solution)/shard_map/ppermute | solution.py:15
  108.7 1.4 %collective-permute-start.31 = (f32[48,16]{1,0:T(8,128)S(1)}, f32[48,16]{1,0:T(8,128)S(1)}, u32[]{:S(2)}, u32[]{:S(2)}) collective-permute-start(f32[48,16]{1,0:T(8,128)S(1)} %add.55), channel_id=1, source_target_pairs={{0,8},{4,12},{8,0},{12,4},{16,24},{20,28},{24,16},{28,20},{1,9},{5... | collective-permute-start | bytes 9224 | tf_op jit(solution)/shard_map/ppermute | solution.py:15
  110.1 2.1 %collective-permute-start.32 = (f32[48,16]{1,0:T(8,128)S(1)}, f32[48,16]{1,0:T(8,128)S(1)}, u32[]{:S(2)}, u32[]{:S(2)}) collective-permute-start(f32[48,16]{1,0:T(8,128)S(1)} %add.55), channel_id=1, source_target_pairs={{0,16},{4,20},{8,24},{12,28},{16,0},{20,4},{24,8},{28,12},{1,17},{... | collective-permute-start | bytes 9224 | tf_op jit(solution)/shard_map/ppermute | solution.py:15
  113.0 2.0 %collective-permute-done.32 = f32[48,16]{1,0:T(8,128)S(1)} collective-permute-done((f32[48,16]{1,0:T(8,128)S(1)}, f32[48,16]{1,0:T(8,128)S(1)}, u32[]{:S(2)}, u32[]{:S(2)}) %collective-permute-start.32) | collective-permute-done | bytes 3104 | tf_op jit(solution)/shard_map/ppermute | solution.py:15
  115.1 2.7 %collective-permute-done.33 = f32[48,16]{1,0:T(8,128)S(1)} collective-permute-done((f32[48,16]{1,0:T(8,128)S(1)}, f32[48,16]{1,0:T(8,128)S(1)}, u32[]{:S(2)}, u32[]{:S(2)}) %collective-permute-start.33) | collective-permute-done | bytes 3104 | tf_op jit(solution)/shard_map/ppermute | solution.py:15
  117.8 1.5 %collective-permute-start.34 = (f32[48,16]{1,0:T(8,128)S(1)}, f32[48,16]{1,0:T(8,128)S(1)}, u32[]{:S(2)}, u32[]{:S(2)}) collective-permute-start(f32[48,16]{1,0:T(8,128)S(1)} %add_add_fusion.1), channel_id=1, source_target_pairs={{0,1},{1,0},{2,3},{3,2},{4,5},{5,4},{6,7},{7,6},{8,9},{9,8},{10,11... | collective-permute-start | bytes 9224 | tf_op jit(solution)/shard_map/ppermute | solution.py:15
  119.3 1.5 %collective-permute-start.35 = (f32[48,16]{1,0:T(8,128)S(1)}, f32[48,16]{1,0:T(8,128)S(1)}, u32[]{:S(2)}, u32[]{:S(2)}) collective-permute-start(f32[48,16]{1,0:T(8,128)S(1)} %add_add_fusion.1), channel_id=1, source_target_pairs={{0,2},{1,3},{2,0},{3,1},{4,6},{5,7},{6,4},{7,5},{8,10},{9,11},{10,... | collective-permute-start | bytes 9224 | tf_op jit(solution)/shard_map/ppermute | solution.py:15
  123.1 2.4 %collective-permute-done.36 = f32[48,16]{1,0:T(8,128)S(1)} collective-permute-done((f32[48,16]{1,0:T(8,128)S(1)}, f32[48,16]{1,0:T(8,128)S(1)}, u32[]{:S(2)}, u32[]{:S(2)}) %collective-permute-start.36) | collective-permute-done | bytes 3104 | tf_op jit(solution)/shard_map/ppermute | solution.py:15
  (76 shorter events, 22.2 us)
Async XLA Ops:
  0.0 11.4 %collective-permute-start.14 = (bf16[2,16,25088]{2,1,0:T(8,128)(2,1)}, bf16[2,16,25088]{2,1,0:T(8,128)(2,1)S(1)}, u32[]{:S(2)}, u32[]{:S(2)}) collective-permute-start(bf16[2,16,25088]{2,1,0:T(8,128)(2,1)} %mine_ref.1), channel_id=1, source_target_pairs={{0,4},{4,0},{8,12},{12,8},{16,20},{20,16},{24,28},{28,24},{1,5},{5... | collective-permute-start | bytes 4816904 | tf_op jit(solution)/shard_map/ppermute | solution.py:15
  1.4 5.7 %collective-permute-start.12 = (bf16[4,1,2,16,128]{4,0,3,2,1:T(4,128)(2,1)S(1)}, bf16[4,1,2,16,128]{4,0,3,2,1:T(4,128)(2,1)S(1)}, u32[]{:S(2)}, u32[]{:S(2)}) collective-permute-start(bf16[4,1,2,16,128]{4,0,3,2,1:T(4,128)(2,1)S(1)} %get-tuple-element.48), channel_id=1, source_target_pairs={{0,16},{4,20},{8,24},{12,28},{16,0},{20,4},{24,8},{28,12},{1,17},{... | collective-permute-start | bytes 98312 | tf_op jit(solution)/shard_map/ppermute | solution.py:15
  7.3 4.0 %collective-permute-start.13 = (bf16[2,2,2,16,128]{4,0,3,2,1:T(2,128)(2,1)S(1)}, bf16[2,2,2,16,128]{4,0,3,2,1:T(2,128)(2,1)S(1)}, u32[]{:S(2)}, u32[]{:S(2)}) collective-permute-start(bf16[2,2,2,16,128]{4,0,3,2,1:T(2,128)(2,1)S(1)} %get-tuple-element.46), channel_id=1, source_target_pairs={{0,8},{4,12},{8,0},{12,4},{16,24},{20,28},{24,16},{28,20},{1,9},{5... | collective-permute-start | bytes 98312 | tf_op jit(solution)/shard_map/ppermute | solution.py:15
  14.3 14.3 %collective-permute-start.18 = (bf16[16,25088]{1,0:T(8,128)(2,1)}, bf16[16,25088]{1,0:T(8,128)(2,1)S(1)}, u32[]{:S(2)}, u32[]{:S(2)}) collective-permute-start(bf16[16,25088]{1,0:T(8,128)(2,1)} %get-tuple-element.40.refs_3_), channel_id=1, source_target_pairs={{4,12},{12,20},{20,28},{8,0},{16,8},{24,16},{5,13},{13,21},{21,29}... | collective-permute-start | bytes 2408456 | tf_op jit(solution)/shard_map/ppermute | solution.py:205
  15.6 21.7 %collective-permute-start.19 = (bf16[16,25088]{1,0:T(8,128)(2,1)}, bf16[16,25088]{1,0:T(8,128)(2,1)}, u32[]{:S(2)}, u32[]{:S(2)}) collective-permute-start(bf16[16,25088]{1,0:T(8,128)(2,1)} %get-tuple-element.41.refs_4_), channel_id=1, source_target_pairs={{4,12},{12,20},{20,28},{8,0},{16,8},{24,16},{5,13},{13,21},{21,29}... | collective-permute-start | bytes 2408456 | tf_op jit(solution)/shard_map/ppermute | solution.py:205
  28.6 21.2 %collective-permute-start.22 = (bf16[16,25088]{1,0:T(8,128)(2,1)S(1)}, bf16[16,25088]{1,0:T(8,128)(2,1)}, u32[]{:S(2)}, u32[]{:S(2)}) collective-permute-start(bf16[16,25088]{1,0:T(8,128)(2,1)S(1)} %collective-permute-done.18.refs_5_), channel_id=1, source_target_pairs={{4,12},{12,20},{20,28},{8,0},{16,8},{24,16},{5,13},{13,21},{21,29}... | collective-permute-start | bytes 2408456 | tf_op jit(solution)/shard_map/ppermute | solution.py:205
  37.3 17.2 %collective-permute-start.23 = (bf16[16,25088]{1,0:T(8,128)(2,1)}, bf16[16,25088]{1,0:T(8,128)(2,1)}, u32[]{:S(2)}, u32[]{:S(2)}) collective-permute-start(bf16[16,25088]{1,0:T(8,128)(2,1)} %collective-permute-done.19.refs_6_), channel_id=1, source_target_pairs={{4,12},{12,20},{20,28},{8,0},{16,8},{24,16},{5,13},{13,21},{21,29}... | collective-permute-start | bytes 2408456 | tf_op jit(solution)/shard_map/ppermute | solution.py:205
  40.4 4.3 %collective-permute-start.16 = (bf16[16,16,128]{2,1,0:T(8,128)(2,1)S(1)}, bf16[16,16,128]{2,1,0:T(8,128)(2,1)S(1)}, u32[]{:S(2)}, u32[]{:S(2)}) collective-permute-start(bf16[16,16,128]{2,1,0:T(8,128)(2,1)S(1)} %bitcast.20), channel_id=1, source_target_pairs={{0,1},{1,0},{2,3},{3,2},{4,5},{5,4},{6,7},{7,6},{8,9},{9,8},{10,11... | collective-permute-start | bytes 196616 | tf_op jit(solution)/shard_map/ppermute | solution.py:15
  44.8 4.3 %collective-permute-start.17 = (bf16[16,16,128]{2,1,0:T(8,128)(2,1)S(1)}, bf16[16,16,128]{2,1,0:T(8,128)(2,1)S(1)}, u32[]{:S(2)}, u32[]{:S(2)}) collective-permute-start(bf16[16,16,128]{2,1,0:T(8,128)(2,1)S(1)} %bitcast_add_fusion), channel_id=1, source_target_pairs={{0,2},{1,3},{2,0},{3,1},{4,6},{5,7},{6,4},{7,5},{8,10},{9,11},{10,... | collective-permute-start | bytes 196616 | tf_op jit(solution)/shard_map/ppermute | solution.py:15
  49.8 24.5 %collective-permute-start.20 = (bf16[16,25088]{1,0:T(8,128)(2,1)S(1)}, bf16[16,25088]{1,0:T(8,128)(2,1)S(1)}, u32[]{:S(2)}, u32[]{:S(2)}) collective-permute-start(bf16[16,25088]{1,0:T(8,128)(2,1)S(1)} %collective-permute-done.18.refs_5_), channel_id=1, source_target_pairs={{0,4},{4,0},{8,12},{12,8},{16,20},{20,16},{24,28},{28,24},{1,5},{5... | collective-permute-start | bytes 2408456 | tf_op jit(solution)/shard_map/ppermute | solution.py:15
  49.8 25.0 %collective-permute-start.26 = (bf16[16,25088]{1,0:T(8,128)(2,1)}, bf16[16,25088]{1,0:T(8,128)(2,1)}, u32[]{:S(2)}, u32[]{:S(2)}) collective-permute-start(bf16[16,25088]{1,0:T(8,128)(2,1)} %collective-permute-done.22.refs_9_), channel_id=1, source_target_pairs={{4,12},{12,20},{20,28},{8,0},{16,8},{24,16},{5,13},{13,21},{21,29}... | collective-permute-start | bytes 2408456 | tf_op jit(solution)/shard_map/ppermute | solution.py:205
  54.5 20.3 %collective-permute-start.27 = (bf16[16,25088]{1,0:T(8,128)(2,1)}, bf16[16,25088]{1,0:T(8,128)(2,1)}, u32[]{:S(2)}, u32[]{:S(2)}) collective-permute-start(bf16[16,25088]{1,0:T(8,128)(2,1)} %collective-permute-done.23.refs_10_), channel_id=1, source_target_pairs={{4,12},{12,20},{20,28},{8,0},{16,8},{24,16},{5,13},{13,21},{21,29}... | collective-permute-start | bytes 2408456 | tf_op jit(solution)/shard_map/ppermute | solution.py:205
  70.9 25.0 %collective-permute-start.21 = (bf16[16,25088]{1,0:T(8,128)(2,1)}, bf16[16,25088]{1,0:T(8,128)(2,1)}, u32[]{:S(2)}, u32[]{:S(2)}) collective-permute-start(bf16[16,25088]{1,0:T(8,128)(2,1)} %collective-permute-done.19.refs_6_), channel_id=1, source_target_pairs={{0,4},{4,0},{8,12},{12,8},{16,20},{20,16},{24,28},{28,24},{1,5},{5... | collective-permute-start | bytes 2408456 | tf_op jit(solution)/shard_map/ppermute | solution.py:15
  74.2 21.7 %collective-permute-start.24 = (bf16[16,25088]{1,0:T(8,128)(2,1)}, bf16[16,25088]{1,0:T(8,128)(2,1)}, u32[]{:S(2)}, u32[]{:S(2)}) collective-permute-start(bf16[16,25088]{1,0:T(8,128)(2,1)} %collective-permute-done.22.refs_9_), channel_id=1, source_target_pairs={{0,4},{4,0},{8,12},{12,8},{16,20},{20,16},{24,28},{28,24},{1,5},{5... | collective-permute-start | bytes 2408456 | tf_op jit(solution)/shard_map/ppermute | solution.py:15
  74.3 21.6 %collective-permute-start.25 = (bf16[16,25088]{1,0:T(8,128)(2,1)}, bf16[16,25088]{1,0:T(8,128)(2,1)S(1)}, u32[]{:S(2)}, u32[]{:S(2)}) collective-permute-start(bf16[16,25088]{1,0:T(8,128)(2,1)} %collective-permute-done.23.refs_10_), channel_id=1, source_target_pairs={{0,4},{4,0},{8,12},{12,8},{16,20},{20,16},{24,28},{28,24},{1,5},{5... | collective-permute-start | bytes 2408456 | tf_op jit(solution)/shard_map/ppermute | solution.py:15
  74.7 21.2 %collective-permute-start.28 = (bf16[16,25088]{1,0:T(8,128)(2,1)}, bf16[16,25088]{1,0:T(8,128)(2,1)}, u32[]{:S(2)}, u32[]{:S(2)}) collective-permute-start(bf16[16,25088]{1,0:T(8,128)(2,1)} %collective-permute-done.26.refs_13_), channel_id=1, source_target_pairs={{0,4},{4,0},{8,12},{12,8},{16,20},{20,16},{24,28},{28,24},{1,5},{5... | collective-permute-start | bytes 2408456 | tf_op jit(solution)/shard_map/ppermute | solution.py:15
  74.8 21.2 %collective-permute-start.29 = (bf16[16,25088]{1,0:T(8,128)(2,1)}, bf16[16,25088]{1,0:T(8,128)(2,1)}, u32[]{:S(2)}, u32[]{:S(2)}) collective-permute-start(bf16[16,25088]{1,0:T(8,128)(2,1)} %collective-permute-done.27.refs_14_), channel_id=1, source_target_pairs={{0,4},{4,0},{8,12},{12,8},{16,20},{20,16},{24,28},{28,24},{1,5},{5... | collective-permute-start | bytes 2408456 | tf_op jit(solution)/shard_map/ppermute | solution.py:15
  106.4 1.5 %collective-permute-start.30 = (f32[48,16]{1,0:T(8,128)}, f32[48,16]{1,0:T(8,128)S(1)}, u32[]{:S(2)}, u32[]{:S(2)}) collective-permute-start(f32[48,16]{1,0:T(8,128)} %get-tuple-element.52), channel_id=1, source_target_pairs={{0,4},{4,0},{8,12},{12,8},{16,20},{20,16},{24,28},{28,24},{1,5},{5... | collective-permute-start | bytes 9224 | tf_op jit(solution)/shard_map/ppermute | solution.py:15
  108.7 4.4 %collective-permute-start.31 = (f32[48,16]{1,0:T(8,128)S(1)}, f32[48,16]{1,0:T(8,128)S(1)}, u32[]{:S(2)}, u32[]{:S(2)}) collective-permute-start(f32[48,16]{1,0:T(8,128)S(1)} %add.55), channel_id=1, source_target_pairs={{0,8},{4,12},{8,0},{12,4},{16,24},{20,28},{24,16},{28,20},{1,9},{5... | collective-permute-start | bytes 9224 | tf_op jit(solution)/shard_map/ppermute | solution.py:15
  110.1 5.0 %collective-permute-start.32 = (f32[48,16]{1,0:T(8,128)S(1)}, f32[48,16]{1,0:T(8,128)S(1)}, u32[]{:S(2)}, u32[]{:S(2)}) collective-permute-start(f32[48,16]{1,0:T(8,128)S(1)} %add.55), channel_id=1, source_target_pairs={{0,16},{4,20},{8,24},{12,28},{16,0},{20,4},{24,8},{28,12},{1,17},{... | collective-permute-start | bytes 9224 | tf_op jit(solution)/shard_map/ppermute | solution.py:15
  112.1 5.6 %collective-permute-start.33 = (f32[48,16]{1,0:T(8,128)S(1)}, f32[48,16]{1,0:T(8,128)S(1)}, u32[]{:S(2)}, u32[]{:S(2)}) collective-permute-start(f32[48,16]{1,0:T(8,128)S(1)} %add.55), channel_id=1, source_target_pairs={{0,24},{4,28},{8,16},{12,20},{16,8},{20,12},{24,0},{28,4},{1,25},{... | collective-permute-start | bytes 9224 | tf_op jit(solution)/shard_map/ppermute | solution.py:15
  117.8 4.1 %collective-permute-start.34 = (f32[48,16]{1,0:T(8,128)S(1)}, f32[48,16]{1,0:T(8,128)S(1)}, u32[]{:S(2)}, u32[]{:S(2)}) collective-permute-start(f32[48,16]{1,0:T(8,128)S(1)} %add_add_fusion.1), channel_id=1, source_target_pairs={{0,1},{1,0},{2,3},{3,2},{4,5},{5,4},{6,7},{7,6},{8,9},{9,8},{10,11... | collective-permute-start | bytes 9224 | tf_op jit(solution)/shard_map/ppermute | solution.py:15
  119.3 3.8 %collective-permute-start.35 = (f32[48,16]{1,0:T(8,128)S(1)}, f32[48,16]{1,0:T(8,128)S(1)}, u32[]{:S(2)}, u32[]{:S(2)}) collective-permute-start(f32[48,16]{1,0:T(8,128)S(1)} %add_add_fusion.1), channel_id=1, source_target_pairs={{0,2},{1,3},{2,0},{3,1},{4,6},{5,7},{6,4},{7,5},{8,10},{9,11},{10,... | collective-permute-start | bytes 9224 | tf_op jit(solution)/shard_map/ppermute | solution.py:15
  120.8 4.7 %collective-permute-start.36 = (f32[48,16]{1,0:T(8,128)S(1)}, f32[48,16]{1,0:T(8,128)S(1)}, u32[]{:S(2)}, u32[]{:S(2)}) collective-permute-start(f32[48,16]{1,0:T(8,128)S(1)} %add_add_fusion.1), channel_id=1, source_target_pairs={{0,3},{1,2},{2,1},{3,0},{4,7},{5,6},{6,5},{7,4},{8,11},{9,10},{10,... | collective-permute-start | bytes 9224 | tf_op jit(solution)/shard_map/ppermute | solution.py:15
  (9 other events, 255.1 us)

commit v2 on v1

--- a/solution.py
+++ b/solution.py
@@ -62,7 +62,7 @@
     width = tile_width(amp.shape[1], 1792)
     first, steps = piece
     cols = steps * width
-    inner = tile_width(width, 896)
+    inner = tile_width(width, 1792)
     return pl.pallas_call(
         functools.partial(fold_kernel, inner=inner),
         grid=(steps,),
@@ -220,9 +220,13 @@
         spare = jnp.zeros((n_ga - local // depth,) + pieces.shape[1:], pieces.dtype)
         pieces = jnp.concatenate([pieces, spare])
         pieces = jnp.roll(pieces, my_col * per_block, axis=0)
-    pieces = pieces[:, None]
+    pieces = pieces.reshape((n_ga // 2, 2) + pieces.shape[1:])
+    upper = my_row % 2 != 0
+    got = flip(jnp.where(upper, pieces[:, 0], pieces[:, 1]), "ga", n_ga, 1)
+    keep = jnp.where(upper, pieces[:, 1], pieces[:, 0])
+    pieces = jnp.stack([jnp.where(upper, got, keep), jnp.where(upper, keep, got)], axis=1)
     bit = n_ga // 2
-    while bit:
+    while bit > 1:
         upper = (my_row & bit) != 0
         half = pieces.shape[0] // 2
         keep = jnp.where(upper, pieces[half:], pieces[:half])
@@ -231,12 +235,11 @@
         pieces = jnp.where(
             upper, jnp.concatenate([got, keep], axis=1), jnp.concatenate([keep, got], axis=1)
         )
-        if bit == min(2, n_ga // 2):
-            pieces, lanes = lax.optimization_barrier((pieces, lanes))
         bit //= 2
+    pieces, lanes = lax.optimization_barrier((pieces, lanes))
     bits = n_ga.bit_length() - 1
     order = pieces[0].reshape((2,) * bits + pieces.shape[2:])
-    order = jnp.transpose(order, tuple(reversed(range(bits))) + tuple(range(bits, order.ndim)))
+    order = jnp.transpose(order, tuple(reversed(range(bits - 1))) + tuple(range(bits - 1, order.ndim)))
     order = order.reshape((n_ga * held, states, depth))
     here = my_col == (my_row * depth) // cols
     rows = jnp.where(here, order, jnp.zeros((), matel.dtype))
@@ -278,7 +281,7 @@
     detuning = energies[:, None] - level[None, :]
     blocks = cols // tile_width(cols, 1792)
     early = max(1, blocks // 7)
-    middle = (blocks - early) // 2
+    middle = max(1, (blocks - early) * 5 // 12)
     halves = []
     for number, piece in enumerate(((0, early), (early, middle), (early + middle, blocks - early - middle))):
         halves.append(fold(index, detuning * detuning, rows, pole_amp, pole_freq, piece))

time: 127 us -> 127 us (level)
  waiting for transfers between devices: 38.6 us -> 42.1 us
  Pallas kernels: 48.2 us -> 46.2 us
  other arithmetic: 6.87 us -> 5.59 us
    pallas_call x3, Pallas kernels: 35.7 us -> 33.8 us  [fold(): pl.pallas_call(functools.partial(fold_kernel, inner=inner), grid=(steps,)...]
    ppermute x6, waiting for transfers between devices: 22.5 us -> 24.4 us  [spread(): hopped.append(lax.ppermute(lane, 'ga', line))]
    ppermute x19, waiting for transfers between devices: 16.1 us -> 17.7 us  [flip(): return lax.ppermute(values, axis, [(i, i ^ bit) for i in range(size)])]
  transfers between devices with their start and end apart: 25 -> 25, of which waited for: 14 -> 14; matrix products, arithmetic and copies ran while one was open for 5% -> 4% of each run, Pallas kernels for 28% -> 27%
where the time goes in v2:
time: 127 us
  Pallas kernels  46.2 us (36%)
  waiting for transfers between devices  42.1 us (33%)
  starting transfers between devices  30 us (24%)
  other arithmetic  5.59 us (4%)
  local copies, waits for them, and re-layouts  1.99 us (2%)
    pallas_call x3, Pallas kernels, fold(): pl.pallas_call(functools.partial(fold_kernel, inner=inner), grid=(steps,)...  33.8 us
    ppermute x6, waiting for transfers between devices, spread(): hopped.append(lax.ppermute(lane, 'ga', line))  24.4 us
    ppermute x19, starting transfers between devices, flip(): return lax.ppermute(values, axis, [(i, i ^ bit) for i in range(size)])  22.3 us
    ppermute x19, waiting for transfers between devices, flip(): return lax.ppermute(values, axis, [(i, i ^ bit) for i in range(size)])  17.7 us
    pallas_call x1, Pallas kernels, close(): pl.pallas_call(functools.partial(close_kernel, window=bands, pieces=piece...  9.5 us
    ppermute x6, starting transfers between devices, spread(): hopped.append(lax.ppermute(lane, 'ga', line))  7.71 us
    pallas_call x1, Pallas kernels, pick(): pl.pallas_call(functools.partial(pick_kernel, base=base, at=at, me=me), i...  2.89 us
  transfers between devices with their start and end apart: 25, of which 14 were waited for; matrix products, arithmetic and copies ran while one was open for 4% of the time, Pallas kernels for 27%

profile of v2, /device:TPU:0, one launch (start us, length us, event | category | flops | bytes accessed | tf_op | source)
XLA Modules:
  0.0 126.8 jit_solution(7159277627777304786)
XLA Ops:
  3.9 4.0 %collective-permute-start.13 = (bf16[2,2,2,16,128]{4,3,2,0,1:T(8,128)(2,1)S(1)}, bf16[2,2,2,16,128]{4,3,2,0,1:T(8,128)(2,1)S(1)}, u32[]{:S(2)}, u32[]{:S(2)}) collective-permute-start(bf16[2,2,2,16,128]{4,3,2,0,1:T(8,128)(2,1)S(1)} %get-tuple-element.48), channel_id=1, source_target_pairs={{0,16},{4,20},{8,24},{12,28},{16,0},{20,4},{24,8},{28,12},{1,17},{... | collective-permute-start | bytes 98312 | tf_op jit(solution)/shard_map/ppermute | solution.py:15
  8.1 1.7 %collective-permute-done.13 = bf16[2,2,2,16,128]{4,3,2,0,1:T(8,128)(2,1)S(1)} collective-permute-done((bf16[2,2,2,16,128]{4,3,2,0,1:T(8,128)(2,1)S(1)}, bf16[2,2,2,16,128]{4,3,2,0,1:T(8,128)(2,1)S(1)}, u32[]{:S(2)}, u32[]{:S(2)}) %collective-permute-start.13) | collective-permute-done | bytes 32800 | tf_op jit(solution)/shard_map/ppermute | solution.py:15
  9.8 2.0 %collective-permute-start.14 = (bf16[1,4,2,16,128]{4,3,2,0,1:T(8,128)(2,1)S(1)}, bf16[1,4,2,16,128]{4,3,2,0,1:T(8,128)(2,1)S(1)}, u32[]{:S(2)}, u32[]{:S(2)}) collective-permute-start(bf16[1,4,2,16,128]{4,3,2,0,1:T(8,128)(2,1)S(1)} %get-tuple-element.46), channel_id=1, source_target_pairs={{0,8},{4,12},{8,0},{12,4},{16,24},{20,28},{24,16},{28,20},{1,9},{5... | collective-permute-start | bytes 98312 | tf_op jit(solution)/shard_map/ppermute | solution.py:15
  12.0 1.8 %collective-permute-done.14 = bf16[1,4,2,16,128]{4,3,2,0,1:T(8,128)(2,1)S(1)} collective-permute-done((bf16[1,4,2,16,128]{4,3,2,0,1:T(8,128)(2,1)S(1)}, bf16[1,4,2,16,128]{4,3,2,0,1:T(8,128)(2,1)S(1)}, u32[]{:S(2)}, u32[]{:S(2)}) %collective-permute-start.14) | collective-permute-done | bytes 32800 | tf_op jit(solution)/shard_map/ppermute | solution.py:15
  13.8 2.9 %pick.3 = (bf16[16,25088]{1,0:T(8,128)(2,1)}, bf16[16,25088]{1,0:T(8,128)(2,1)}) custom-call(s32[16]{0:T(128)S(1)} %concatenate.31.info_ref, bf16[2,16,25088]{2,1,0:T(8,128)(2,1)} %mine_ref.1, bf16[2,16,25088]{2,1,0:T(8,128)(2,1)S(1)} %collective-permute-done.15.other_ref), custom_call_target="tpu_custom_call" | custom-call | tf_op jit(solution)/shard_map/pick/pallas_call | solution.py:107
  19.3 11.8 %collective-permute-done.18.refs_5_ = bf16[16,25088]{1,0:T(8,128)(2,1)S(1)} collective-permute-done((bf16[16,25088]{1,0:T(8,128)(2,1)}, bf16[16,25088]{1,0:T(8,128)(2,1)S(1)}, u32[]{:S(2)}, u32[]{:S(2)}) %collective-permute-start.18) | collective-permute-done | bytes 802848 | tf_op jit(solution)/shard_map/ppermute | solution.py:205
  32.4 7.4 %collective-permute-done.19.refs_6_ = bf16[16,25088]{1,0:T(8,128)(2,1)} collective-permute-done((bf16[16,25088]{1,0:T(8,128)(2,1)}, bf16[16,25088]{1,0:T(8,128)(2,1)}, u32[]{:S(2)}, u32[]{:S(2)}) %collective-permute-start.19) | collective-permute-done | bytes 802848 | tf_op jit(solution)/shard_map/ppermute | solution.py:205
  41.2 2.1 %collective-permute-start.16 = (bf16[16,16,128]{2,1,0:T(8,128)(2,1)S(1)}, bf16[16,16,128]{2,1,0:T(8,128)(2,1)S(1)}, u32[]{:S(2)}, u32[]{:S(2)}) collective-permute-start(bf16[16,16,128]{2,1,0:T(8,128)(2,1)S(1)} %bitcast.32), channel_id=1, source_target_pairs={{0,1},{1,0},{2,3},{3,2},{4,5},{5,4},{6,7},{7,6},{8,9},{9,8},{10,11... | collective-permute-start | bytes 196616 | tf_op jit(solution)/shard_map/ppermute | solution.py:15
  43.5 2.1 %collective-permute-done.16 = bf16[16,16,128]{2,1,0:T(8,128)(2,1)S(1)} collective-permute-done((bf16[16,16,128]{2,1,0:T(8,128)(2,1)S(1)}, bf16[16,16,128]{2,1,0:T(8,128)(2,1)S(1)}, u32[]{:S(2)}, u32[]{:S(2)}) %collective-permute-start.16) | collective-permute-done | bytes 65568 | tf_op jit(solution)/shard_map/ppermute | solution.py:15
  45.6 2.1 %collective-permute-start.17 = (bf16[16,16,128]{2,1,0:T(8,128)(2,1)S(1)}, bf16[16,16,128]{2,1,0:T(8,128)(2,1)S(1)}, u32[]{:S(2)}, u32[]{:S(2)}) collective-permute-start(bf16[16,16,128]{2,1,0:T(8,128)(2,1)S(1)} %bitcast_add_fusion), channel_id=1, source_target_pairs={{0,2},{1,3},{2,0},{3,1},{4,6},{5,7},{6,4},{7,5},{8,10},{9,11},{10,... | collective-permute-start | bytes 196616 | tf_op jit(solution)/shard_map/ppermute | solution.py:15
  51.9 5.2 %collective-permute-done.23.refs_10_ = bf16[16,25088]{1,0:T(8,128)(2,1)} collective-permute-done((bf16[16,25088]{1,0:T(8,128)(2,1)}, bf16[16,25088]{1,0:T(8,128)(2,1)}, u32[]{:S(2)}, u32[]{:S(2)}) %collective-permute-start.23) | collective-permute-done | bytes 802848 | tf_op jit(solution)/shard_map/ppermute | solution.py:205
  58.3 16.3 %fold.5.refs_2_ = bf16[5,48,12544]{2,1,0:T(8,128)(2,1)} custom-call(s32[5]{0:T(128)} %copy-done.19, f32[3,5]{1,0:T(4,128)} %subtract_multiply_fusion.detuning_ref, bf16[16,16,128]{2,1,0:T(8,128)(2,1)} %add.55.rows_ref, bf16[128,25088]{1,0:T(8,128)(2,1)} %amp_ref.5, bf16[128,25088]{1,0:T(8,128)(2,1)} %freq_ref.5), custom_call_target="tpu_custom_call" | custom-call | flops 24000000000 | bytes 3211264 | tf_op jit(solution)/shard_map/fold/pallas_call | solution.py:66
  74.6 1.6 %collective-permute-start.21 = (bf16[16,25088]{1,0:T(8,128)(2,1)}, bf16[16,25088]{1,0:T(8,128)(2,1)}, u32[]{:S(2)}, u32[]{:S(2)}) collective-permute-start(bf16[16,25088]{1,0:T(8,128)(2,1)} %collective-permute-done.19.refs_6_), channel_id=1, source_target_pairs={{0,4},{4,0},{8,12},{12,8},{16,20},{20,16},{24,28},{28,24},{1,5},{5... | collective-permute-start | bytes 2408456 | tf_op jit(solution)/shard_map/ppermute | solution.py:15
  77.2 12.3 %fold.4.refs_1_ = bf16[5,48,8960]{2,1,0:T(8,128)(2,1)} custom-call(s32[5]{0:T(128)} %copy-done.19, f32[3,5]{1,0:T(4,128)} %subtract_multiply_fusion.detuning_ref, bf16[16,16,128]{2,1,0:T(8,128)(2,1)} %add.55.rows_ref, bf16[128,25088]{1,0:T(8,128)(2,1)} %amp_ref.5, bf16[128,25088]{1,0:T(8,128)(2,1)} %freq_ref.5), custom_call_target="tpu_custom_call" | custom-call | flops 17142856704 | bytes 2293760 | tf_op jit(solution)/shard_map/fold/pallas_call | solution.py:66
  89.5 5.3 %fold.3.refs_0_ = bf16[5,48,3584]{2,1,0:T(8,128)(2,1)S(1)} custom-call(s32[5]{0:T(128)} %copy-done.19, f32[3,5]{1,0:T(4,128)} %subtract_multiply_fusion.detuning_ref, bf16[16,16,128]{2,1,0:T(8,128)(2,1)} %add.55.rows_ref, bf16[128,25088]{1,0:T(8,128)(2,1)} %amp_ref.5, bf16[128,25088]{1,0:T(8,128)(2,1)} %freq_ref.5), custom_call_target="tpu_custom_call" | custom-call | flops 6857142784 | bytes 917504 | tf_op jit(solution)/shard_map/fold/pallas_call | solution.py:66
  95.8 9.5 %close.3 = f32[48,16]{1,0:T(8,128)} custom-call(s32[16]{0:T(128)} %copy-done.17, bf16[5,48,3584]{2,1,0:T(8,128)(2,1)S(1)} %fold.3.refs_0_, bf16[5,48,8960]{2,1,0:T(8,128)(2,1)} %fold.4.refs_1_, bf16[5,48,12544]{2,1,0:T(8,128)(2,1)} %fold.5.refs_2_, bf16[16,25088]{1,0:T(8,128)(2,1)} %get-tuple-element.40.refs_3_, ...), custom_call_target="tpu_custom_call" | custom-call | tf_op jit(solution)/shard_map/close/pallas_call | solution.py:180
  105.4 1.4 %collective-permute-done.30 = f32[48,16]{1,0:T(8,128)S(1)} collective-permute-done((f32[48,16]{1,0:T(8,128)}, f32[48,16]{1,0:T(8,128)S(1)}, u32[]{:S(2)}, u32[]{:S(2)}) %collective-permute-start.30) | collective-permute-done | bytes 3104 | tf_op jit(solution)/shard_map/ppermute | solution.py:15
  107.5 1.5 %collective-permute-start.31 = (f32[48,16]{1,0:T(8,128)S(1)}, f32[48,16]{1,0:T(8,128)S(1)}, u32[]{:S(2)}, u32[]{:S(2)}) collective-permute-start(f32[48,16]{1,0:T(8,128)S(1)} %add.56), channel_id=1, source_target_pairs={{0,8},{4,12},{8,0},{12,4},{16,24},{20,28},{24,16},{28,20},{1,9},{5... | collective-permute-start | bytes 9224 | tf_op jit(solution)/shard_map/ppermute | solution.py:15
  109.1 3.7 %collective-permute-start.32 = (f32[48,16]{1,0:T(8,128)S(1)}, f32[48,16]{1,0:T(8,128)S(1)}, u32[]{:S(2)}, u32[]{:S(2)}) collective-permute-start(f32[48,16]{1,0:T(8,128)S(1)} %add.56), channel_id=1, source_target_pairs={{0,16},{4,20},{8,24},{12,28},{16,0},{20,4},{24,8},{28,12},{1,17},{... | collective-permute-start | bytes 9224 | tf_op jit(solution)/shard_map/ppermute | solution.py:15
  112.8 1.9 %collective-permute-done.32 = f32[48,16]{1,0:T(8,128)S(1)} collective-permute-done((f32[48,16]{1,0:T(8,128)S(1)}, f32[48,16]{1,0:T(8,128)S(1)}, u32[]{:S(2)}, u32[]{:S(2)}) %collective-permute-start.32) | collective-permute-done | bytes 3104 | tf_op jit(solution)/shard_map/ppermute | solution.py:15
  114.7 3.7 %collective-permute-done.33 = f32[48,16]{1,0:T(8,128)S(1)} collective-permute-done((f32[48,16]{1,0:T(8,128)S(1)}, f32[48,16]{1,0:T(8,128)S(1)}, u32[]{:S(2)}, u32[]{:S(2)}) %collective-permute-start.33) | collective-permute-done | bytes 3104 | tf_op jit(solution)/shard_map/ppermute | solution.py:15
  118.4 1.6 %collective-permute-start.34 = (f32[48,16]{1,0:T(8,128)S(1)}, f32[48,16]{1,0:T(8,128)S(1)}, u32[]{:S(2)}, u32[]{:S(2)}) collective-permute-start(f32[48,16]{1,0:T(8,128)S(1)} %add_add_fusion.1), channel_id=1, source_target_pairs={{0,1},{1,0},{2,3},{3,2},{4,5},{5,4},{6,7},{7,6},{8,9},{9,8},{10,11... | collective-permute-start | bytes 9224 | tf_op jit(solution)/shard_map/ppermute | solution.py:15
  120.0 1.5 %collective-permute-start.35 = (f32[48,16]{1,0:T(8,128)S(1)}, f32[48,16]{1,0:T(8,128)S(1)}, u32[]{:S(2)}, u32[]{:S(2)}) collective-permute-start(f32[48,16]{1,0:T(8,128)S(1)} %add_add_fusion.1), channel_id=1, source_target_pairs={{0,2},{1,3},{2,0},{3,1},{4,6},{5,7},{6,4},{7,5},{8,10},{9,11},{10,... | collective-permute-start | bytes 9224 | tf_op jit(solution)/shard_map/ppermute | solution.py:15
  123.8 2.4 %collective-permute-done.36 = f32[48,16]{1,0:T(8,128)S(1)} collective-permute-done((f32[48,16]{1,0:T(8,128)S(1)}, f32[48,16]{1,0:T(8,128)S(1)}, u32[]{:S(2)}, u32[]{:S(2)}) %collective-permute-start.36) | collective-permute-done | bytes 3104 | tf_op jit(solution)/shard_map/ppermute | solution.py:15
  (79 shorter events, 20.2 us)
Async XLA Ops:
  0.0 13.8 %collective-permute-start.15 = (bf16[2,16,25088]{2,1,0:T(8,128)(2,1)}, bf16[2,16,25088]{2,1,0:T(8,128)(2,1)S(1)}, u32[]{:S(2)}, u32[]{:S(2)}) collective-permute-start(bf16[2,16,25088]{2,1,0:T(8,128)(2,1)} %mine_ref.1), channel_id=1, source_target_pairs={{0,4},{4,0},{8,12},{12,8},{16,20},{20,16},{24,28},{28,24},{1,5},{5... | collective-permute-start | bytes 4816904 | tf_op jit(solution)/shard_map/ppermute | solution.py:15
  1.4 2.4 %collective-permute-start.12 = (bf16[4,2,16,128]{3,2,1,0:T(8,128)(2,1)S(1)}, bf16[4,2,16,128]{3,2,1,0:T(8,128)(2,1)S(1)}, u32[]{:S(2)}, u32[]{:S(2)}) collective-permute-start(bf16[4,2,16,128]{3,2,1,0:T(8,128)(2,1)S(1)} %select_bitcast_fusion), channel_id=1, source_target_pairs={{0,4},{4,0},{8,12},{12,8},{16,20},{20,16},{24,28},{28,24},{1,5},{5... | collective-permute-start | bytes 98312 | tf_op jit(solution)/shard_map/ppermute | solution.py:15
  3.9 5.9 %collective-permute-start.13 = (bf16[2,2,2,16,128]{4,3,2,0,1:T(8,128)(2,1)S(1)}, bf16[2,2,2,16,128]{4,3,2,0,1:T(8,128)(2,1)S(1)}, u32[]{:S(2)}, u32[]{:S(2)}) collective-permute-start(bf16[2,2,2,16,128]{4,3,2,0,1:T(8,128)(2,1)S(1)} %get-tuple-element.48), channel_id=1, source_target_pairs={{0,16},{4,20},{8,24},{12,28},{16,0},{20,4},{24,8},{28,12},{1,17},{... | collective-permute-start | bytes 98312 | tf_op jit(solution)/shard_map/ppermute | solution.py:15
  9.8 4.0 %collective-permute-start.14 = (bf16[1,4,2,16,128]{4,3,2,0,1:T(8,128)(2,1)S(1)}, bf16[1,4,2,16,128]{4,3,2,0,1:T(8,128)(2,1)S(1)}, u32[]{:S(2)}, u32[]{:S(2)}) collective-permute-start(bf16[1,4,2,16,128]{4,3,2,0,1:T(8,128)(2,1)S(1)} %get-tuple-element.46), channel_id=1, source_target_pairs={{0,8},{4,12},{8,0},{12,4},{16,24},{20,28},{24,16},{28,20},{1,9},{5... | collective-permute-start | bytes 98312 | tf_op jit(solution)/shard_map/ppermute | solution.py:15
  16.7 14.4 %collective-permute-start.18 = (bf16[16,25088]{1,0:T(8,128)(2,1)}, bf16[16,25088]{1,0:T(8,128)(2,1)S(1)}, u32[]{:S(2)}, u32[]{:S(2)}) collective-permute-start(bf16[16,25088]{1,0:T(8,128)(2,1)} %get-tuple-element.40.refs_3_), channel_id=1, source_target_pairs={{4,12},{12,20},{20,28},{8,0},{16,8},{24,16},{5,13},{13,21},{21,29}... | collective-permute-start | bytes 2408456 | tf_op jit(solution)/shard_map/ppermute | solution.py:205
  18.0 21.8 %collective-permute-start.19 = (bf16[16,25088]{1,0:T(8,128)(2,1)}, bf16[16,25088]{1,0:T(8,128)(2,1)}, u32[]{:S(2)}, u32[]{:S(2)}) collective-permute-start(bf16[16,25088]{1,0:T(8,128)(2,1)} %get-tuple-element.41.refs_4_), channel_id=1, source_target_pairs={{4,12},{12,20},{20,28},{8,0},{16,8},{24,16},{5,13},{13,21},{21,29}... | collective-permute-start | bytes 2408456 | tf_op jit(solution)/shard_map/ppermute | solution.py:205
  31.1 19.4 %collective-permute-start.22 = (bf16[16,25088]{1,0:T(8,128)(2,1)S(1)}, bf16[16,25088]{1,0:T(8,128)(2,1)}, u32[]{:S(2)}, u32[]{:S(2)}) collective-permute-start(bf16[16,25088]{1,0:T(8,128)(2,1)S(1)} %collective-permute-done.18.refs_5_), channel_id=1, source_target_pairs={{4,12},{12,20},{20,28},{8,0},{16,8},{24,16},{5,13},{13,21},{21,29}... | collective-permute-start | bytes 2408456 | tf_op jit(solution)/shard_map/ppermute | solution.py:205
  39.8 17.2 %collective-permute-start.23 = (bf16[16,25088]{1,0:T(8,128)(2,1)}, bf16[16,25088]{1,0:T(8,128)(2,1)}, u32[]{:S(2)}, u32[]{:S(2)}) collective-permute-start(bf16[16,25088]{1,0:T(8,128)(2,1)} %collective-permute-done.19.refs_6_), channel_id=1, source_target_pairs={{4,12},{12,20},{20,28},{8,0},{16,8},{24,16},{5,13},{13,21},{21,29}... | collective-permute-start | bytes 2408456 | tf_op jit(solution)/shard_map/ppermute | solution.py:205
  41.2 4.3 %collective-permute-start.16 = (bf16[16,16,128]{2,1,0:T(8,128)(2,1)S(1)}, bf16[16,16,128]{2,1,0:T(8,128)(2,1)S(1)}, u32[]{:S(2)}, u32[]{:S(2)}) collective-permute-start(bf16[16,16,128]{2,1,0:T(8,128)(2,1)S(1)} %bitcast.32), channel_id=1, source_target_pairs={{0,1},{1,0},{2,3},{3,2},{4,5},{5,4},{6,7},{7,6},{8,9},{9,8},{10,11... | collective-permute-start | bytes 196616 | tf_op jit(solution)/shard_map/ppermute | solution.py:15
  45.6 4.4 %collective-permute-start.17 = (bf16[16,16,128]{2,1,0:T(8,128)(2,1)S(1)}, bf16[16,16,128]{2,1,0:T(8,128)(2,1)S(1)}, u32[]{:S(2)}, u32[]{:S(2)}) collective-permute-start(bf16[16,16,128]{2,1,0:T(8,128)(2,1)S(1)} %bitcast_add_fusion), channel_id=1, source_target_pairs={{0,2},{1,3},{2,0},{3,1},{4,6},{5,7},{6,4},{7,5},{8,10},{9,11},{10,... | collective-permute-start | bytes 196616 | tf_op jit(solution)/shard_map/ppermute | solution.py:15
  50.6 25.7 %collective-permute-start.20 = (bf16[16,25088]{1,0:T(8,128)(2,1)S(1)}, bf16[16,25088]{1,0:T(8,128)(2,1)S(1)}, u32[]{:S(2)}, u32[]{:S(2)}) collective-permute-start(bf16[16,25088]{1,0:T(8,128)(2,1)S(1)} %collective-permute-done.18.refs_5_), channel_id=1, source_target_pairs={{0,4},{4,0},{8,12},{12,8},{16,20},{20,16},{24,28},{28,24},{1,5},{5... | collective-permute-start | bytes 2408456 | tf_op jit(solution)/shard_map/ppermute | solution.py:15
  50.6 26.1 %collective-permute-start.26 = (bf16[16,25088]{1,0:T(8,128)(2,1)}, bf16[16,25088]{1,0:T(8,128)(2,1)}, u32[]{:S(2)}, u32[]{:S(2)}) collective-permute-start(bf16[16,25088]{1,0:T(8,128)(2,1)} %collective-permute-done.22.refs_9_), channel_id=1, source_target_pairs={{4,12},{12,20},{20,28},{8,0},{16,8},{24,16},{5,13},{13,21},{21,29}... | collective-permute-start | bytes 2408456 | tf_op jit(solution)/shard_map/ppermute | solution.py:205
  57.0 19.8 %collective-permute-start.27 = (bf16[16,25088]{1,0:T(8,128)(2,1)}, bf16[16,25088]{1,0:T(8,128)(2,1)}, u32[]{:S(2)}, u32[]{:S(2)}) collective-permute-start(bf16[16,25088]{1,0:T(8,128)(2,1)} %collective-permute-done.23.refs_10_), channel_id=1, source_target_pairs={{4,12},{12,20},{20,28},{8,0},{16,8},{24,16},{5,13},{13,21},{21,29}... | collective-permute-start | bytes 2408456 | tf_op jit(solution)/shard_map/ppermute | solution.py:205
  74.6 20.2 %collective-permute-start.21 = (bf16[16,25088]{1,0:T(8,128)(2,1)}, bf16[16,25088]{1,0:T(8,128)(2,1)}, u32[]{:S(2)}, u32[]{:S(2)}) collective-permute-start(bf16[16,25088]{1,0:T(8,128)(2,1)} %collective-permute-done.19.refs_6_), channel_id=1, source_target_pairs={{0,4},{4,0},{8,12},{12,8},{16,20},{20,16},{24,28},{28,24},{1,5},{5... | collective-permute-start | bytes 2408456 | tf_op jit(solution)/shard_map/ppermute | solution.py:15
  76.2 18.6 %collective-permute-start.24 = (bf16[16,25088]{1,0:T(8,128)(2,1)}, bf16[16,25088]{1,0:T(8,128)(2,1)}, u32[]{:S(2)}, u32[]{:S(2)}) collective-permute-start(bf16[16,25088]{1,0:T(8,128)(2,1)} %collective-permute-done.22.refs_9_), channel_id=1, source_target_pairs={{0,4},{4,0},{8,12},{12,8},{16,20},{20,16},{24,28},{28,24},{1,5},{5... | collective-permute-start | bytes 2408456 | tf_op jit(solution)/shard_map/ppermute | solution.py:15
  76.3 18.5 %collective-permute-start.25 = (bf16[16,25088]{1,0:T(8,128)(2,1)}, bf16[16,25088]{1,0:T(8,128)(2,1)S(1)}, u32[]{:S(2)}, u32[]{:S(2)}) collective-permute-start(bf16[16,25088]{1,0:T(8,128)(2,1)} %collective-permute-done.23.refs_10_), channel_id=1, source_target_pairs={{0,4},{4,0},{8,12},{12,8},{16,20},{20,16},{24,28},{28,24},{1,5},{5... | collective-permute-start | bytes 2408456 | tf_op jit(solution)/shard_map/ppermute | solution.py:15
  76.7 18.1 %collective-permute-start.28 = (bf16[16,25088]{1,0:T(8,128)(2,1)}, bf16[16,25088]{1,0:T(8,128)(2,1)}, u32[]{:S(2)}, u32[]{:S(2)}) collective-permute-start(bf16[16,25088]{1,0:T(8,128)(2,1)} %collective-permute-done.26.refs_13_), channel_id=1, source_target_pairs={{0,4},{4,0},{8,12},{12,8},{16,20},{20,16},{24,28},{28,24},{1,5},{5... | collective-permute-start | bytes 2408456 | tf_op jit(solution)/shard_map/ppermute | solution.py:15
  76.8 18.0 %collective-permute-start.29 = (bf16[16,25088]{1,0:T(8,128)(2,1)}, bf16[16,25088]{1,0:T(8,128)(2,1)}, u32[]{:S(2)}, u32[]{:S(2)}) collective-permute-start(bf16[16,25088]{1,0:T(8,128)(2,1)} %collective-permute-done.27.refs_14_), channel_id=1, source_target_pairs={{0,4},{4,0},{8,12},{12,8},{16,20},{20,16},{24,28},{28,24},{1,5},{5... | collective-permute-start | bytes 2408456 | tf_op jit(solution)/shard_map/ppermute | solution.py:15
  107.5 5.3 %collective-permute-start.31 = (f32[48,16]{1,0:T(8,128)S(1)}, f32[48,16]{1,0:T(8,128)S(1)}, u32[]{:S(2)}, u32[]{:S(2)}) collective-permute-start(f32[48,16]{1,0:T(8,128)S(1)} %add.56), channel_id=1, source_target_pairs={{0,8},{4,12},{8,0},{12,4},{16,24},{20,28},{24,16},{28,20},{1,9},{5... | collective-permute-start | bytes 9224 | tf_op jit(solution)/shard_map/ppermute | solution.py:15
  109.1 5.7 %collective-permute-start.32 = (f32[48,16]{1,0:T(8,128)S(1)}, f32[48,16]{1,0:T(8,128)S(1)}, u32[]{:S(2)}, u32[]{:S(2)}) collective-permute-start(f32[48,16]{1,0:T(8,128)S(1)} %add.56), channel_id=1, source_target_pairs={{0,16},{4,20},{8,24},{12,28},{16,0},{20,4},{24,8},{28,12},{1,17},{... | collective-permute-start | bytes 9224 | tf_op jit(solution)/shard_map/ppermute | solution.py:15
  112.8 5.6 %collective-permute-start.33 = (f32[48,16]{1,0:T(8,128)S(1)}, f32[48,16]{1,0:T(8,128)S(1)}, u32[]{:S(2)}, u32[]{:S(2)}) collective-permute-start(f32[48,16]{1,0:T(8,128)S(1)} %add.56), channel_id=1, source_target_pairs={{0,24},{4,28},{8,16},{12,20},{16,8},{20,12},{24,0},{28,4},{1,25},{... | collective-permute-start | bytes 9224 | tf_op jit(solution)/shard_map/ppermute | solution.py:15
  118.4 4.1 %collective-permute-start.34 = (f32[48,16]{1,0:T(8,128)S(1)}, f32[48,16]{1,0:T(8,128)S(1)}, u32[]{:S(2)}, u32[]{:S(2)}) collective-permute-start(f32[48,16]{1,0:T(8,128)S(1)} %add_add_fusion.1), channel_id=1, source_target_pairs={{0,1},{1,0},{2,3},{3,2},{4,5},{5,4},{6,7},{7,6},{8,9},{9,8},{10,11... | collective-permute-start | bytes 9224 | tf_op jit(solution)/shard_map/ppermute | solution.py:15
  120.0 3.8 %collective-permute-start.35 = (f32[48,16]{1,0:T(8,128)S(1)}, f32[48,16]{1,0:T(8,128)S(1)}, u32[]{:S(2)}, u32[]{:S(2)}) collective-permute-start(f32[48,16]{1,0:T(8,128)S(1)} %add_add_fusion.1), channel_id=1, source_target_pairs={{0,2},{1,3},{2,0},{3,1},{4,6},{5,7},{6,4},{7,5},{8,10},{9,11},{10,... | collective-permute-start | bytes 9224 | tf_op jit(solution)/shard_map/ppermute | solution.py:15
  121.5 4.7 %collective-permute-start.36 = (f32[48,16]{1,0:T(8,128)S(1)}, f32[48,16]{1,0:T(8,128)S(1)}, u32[]{:S(2)}, u32[]{:S(2)}) collective-permute-start(f32[48,16]{1,0:T(8,128)S(1)} %add_add_fusion.1), channel_id=1, source_target_pairs={{0,3},{1,2},{2,1},{3,0},{4,7},{5,6},{6,5},{7,4},{8,11},{9,10},{10,... | collective-permute-start | bytes 9224 | tf_op jit(solution)/shard_map/ppermute | solution.py:15
  (10 other events, 306.7 us)
